TPU v7x, 32 devices: a whole 2x2x4 slice. The times are simulated.
32 devices in a mesh: pipe: 2 (over x), dp: 8 (over z, y), tensor: 2 (over core).
Axes of the slice: x: 2, y: 2, z: 4, core: 2. Of those that a mesh axis runs over, the one named last changes fastest.
Arguments:
- inputs: bfloat16 [2, 8, 256, 1536], P(None, 'dp'), may hold values from -6 to 6
- cotangents: bfloat16 [2, 8, 256, 1536], P(None, 'dp'), may hold values from -6 to 6
- norm_scales: float32 [2, 1536, 2], P('pipe'), may hold values from 0.5 to 1.5
- w_query: bfloat16 [2, 1536, 1536], P('pipe', None, 'tensor'), may hold values from -0.15625 to 0.15625
- key_weight: bfloat16 [2, 1536, 768], P('pipe', None, 'tensor'), may hold values from -0.15625 to 0.15625
- value_weight: bfloat16 [2, 1536, 768], P('pipe', None, 'tensor'), may hold values from -0.15625 to 0.15625
- w_out: bfloat16 [2, 1536, 1536], P('pipe', None, 'tensor'), may hold values from -0.875 to 0.875
- w_gate: bfloat16 [2, 1536, 4096], P('pipe', None, 'tensor'), may hold values from -0.15625 to 0.15625
- w_up: bfloat16 [2, 1536, 4096], P('pipe', None, 'tensor'), may hold values from -0.15625 to 0.15625
- down_weight: bfloat16 [2, 1536, 4096], P('pipe', None, 'tensor'), may hold values from -0.09375 to 0.09375
Outputs:
- section_out: bfloat16 [2, 2, 8, 256, 1536], P('pipe', None, 'dp')
- section_in_grad: bfloat16 [2, 2, 8, 256, 1536], P('pipe', None, 'dp')
- grad_scales: float32 [2, 1536, 2], P('pipe', 'dp')
- grad_query: float32 [2, 1536, 1536], P('pipe', 'dp', 'tensor')
- grad_key: float32 [2, 1536, 768], P('pipe', 'dp', 'tensor')
- value_weight_gradient: float32 [2, 1536, 768], P('pipe', 'dp', 'tensor')
- grad_out: float32 [2, 1536, 1536], P('pipe', 'dp', 'tensor')
- grad_gate: float32 [2, 1536, 4096], P('pipe', 'dp', 'tensor')
- grad_up: float32 [2, 1536, 4096], P('pipe', 'dp', 'tensor')
- grad_down: float32 [2, 1536, 4096], P('pipe', 'dp', 'tensor')
All inputs are finite; a program needn't handle non-finite values.
Results may differ from a plain program's by a relative error of at most 0.03.
Values may be sent and summed in bfloat16 or wider, within the bound.
A program may use at most 256 MiB of HBM per device.

v0:
```python
import jax
import jax.numpy as jnp
from jax import lax
from jax.sharding import PartitionSpec as P

HEAD_SIZE = 96


EPS = 1e-05
THETA = 100000.0


def passed_along(value, axis, by):
    peers = lax.axis_size(axis)
    pairs = [(i, i + by) for i in range(peers) if 0 <= i + by < peers]
    return lax.ppermute(value, axis, pairs)


def rope_tables(length, size):
    positions = jnp.arange(length, dtype=jnp.float32)
    freqs = THETA ** (-(jnp.arange(size // 2, dtype=jnp.float32) * 2.0 / size))
    angles = positions[:, None] * freqs[None, :]
    cosine = jnp.concatenate([jnp.cos(angles), jnp.cos(angles)], axis=-1)
    sine = jnp.concatenate([jnp.sin(angles), jnp.sin(angles)], axis=-1)
    return (cosine[:, None, :], sine[:, None, :])


def rotate(values, cosine, sine):
    half = values.shape[-1] // 2
    turned = jnp.concatenate([-values[..., half:], values[..., :half]], axis=-1)
    return values * cosine + turned * sine


def rotate_back(grads, cosine, sine):
    half = grads.shape[-1] // 2
    moved = grads * sine
    turned = jnp.concatenate([moved[..., half:], -moved[..., :half]], axis=-1)
    return grads * cosine + turned


def times_t(left, right):
    return lax.dot_general(
        left, right, (((1,), (1,)), ((), ())), preferred_element_type=jnp.float32
    )


def over_rows(left, right):
    return lax.dot_general(
        left, right, (((0,), (0,)), ((), ())), preferred_element_type=jnp.float32
    )


def heads_total(partial_value):
    return lax.psum(partial_value.astype(jnp.bfloat16), "tensor").astype(jnp.float32)


def inputs_total(partial_value):
    return lax.psum(partial_value.astype(jnp.bfloat16), "tensor").astype(jnp.float32)


def norm_rows(values, gain):
    scale = lax.rsqrt(jnp.mean(values * values, axis=-1, keepdims=True) + EPS)
    return (scale, (values * scale * gain).astype(jnp.bfloat16))


def score_table(query, keys):
    length = query.shape[0]
    scores = jnp.einsum(
        "qgrd,kgd->grqk", query, keys, preferred_element_type=jnp.float32
    ) * HEAD_SIZE ** (-0.5)
    causal = jnp.arange(length)[:, None] >= jnp.arange(length)[None, :]
    return (scores, causal)


def forward_layer(hidden, params):
    scales, w_query, key_weight, value_weight, w_out, w_gate, w_up, down_weight = params
    length = hidden.shape[0]
    groups = key_weight.shape[1] // HEAD_SIZE
    wide = hidden.astype(jnp.float32)
    scale_one, normed_one = norm_rows(wide, scales[:, 0])
    cosine, sine = rope_tables(length, HEAD_SIZE)
    query = (
        rotate(
            jnp.dot(normed_one, w_query, preferred_element_type=jnp.float32).reshape(
                length, -1, HEAD_SIZE
            ),
            cosine,
            sine,
        )
        .astype(jnp.bfloat16)
        .reshape(length, groups, -1, HEAD_SIZE)
    )
    keys = rotate(
        jnp.dot(normed_one, key_weight, preferred_element_type=jnp.float32).reshape(
            length, groups, HEAD_SIZE
        ),
        cosine,
        sine,
    ).astype(jnp.bfloat16)
    values = (
        jnp.dot(normed_one, value_weight, preferred_element_type=jnp.float32)
        .astype(jnp.bfloat16)
        .reshape(length, groups, HEAD_SIZE)
    )
    scores, causal = score_table(query, keys)
    log_total = jnp.log(jnp.sum(jnp.where(causal, jnp.exp(scores), 0.0), axis=-1))
    probs = jnp.where(causal, jnp.exp(scores - log_total[..., None]), 0.0).astype(jnp.bfloat16)
    mixed = (
        jnp.einsum("grqk,kgd->qgrd", probs, values, preferred_element_type=jnp.float32)
        .astype(jnp.bfloat16)
        .reshape(length, -1)
    )
    middle = wide + heads_total(times_t(mixed, w_out))
    scale_two, normed_two = norm_rows(middle, scales[:, 1])
    gate = jnp.dot(normed_two, w_gate, preferred_element_type=jnp.float32)
    upward = jnp.dot(normed_two, w_up, preferred_element_type=jnp.float32)
    activated = (gate * jax.nn.sigmoid(gate) * upward).astype(jnp.bfloat16)
    result = (middle + heads_total(times_t(activated, down_weight))).astype(jnp.bfloat16)
    record = (
        hidden,
        scale_one,
        normed_one,
        query,
        keys,
        values,
        mixed,
        log_total,
        middle,
        scale_two,
        normed_two,
        gate,
        upward,
        activated,
    )
    return (record, result)


def backward_feedforward(record, cotangent, params):
    (
        hidden,
        scale_one,
        normed_one,
        query,
        keys,
        values,
        mixed,
        log_total,
        middle,
        scale_two,
        normed_two,
        gate,
        upward,
        activated,
    ) = record
    scales, w_query, key_weight, value_weight, w_out, w_gate, w_up, down_weight = params
    grad_down = over_rows(cotangent, activated)
    d_act = jnp.dot(cotangent, down_weight, preferred_element_type=jnp.float32)
    sig = jax.nn.sigmoid(gate)
    d_gate = (d_act * upward * sig * (1.0 + gate * (1.0 - sig))).astype(jnp.bfloat16)
    d_up = (d_act * gate * sig).astype(jnp.bfloat16)
    grad_gate = over_rows(normed_two, d_gate)
    grad_up = over_rows(normed_two, d_up)
    d_normed = inputs_total(times_t(d_gate, w_gate) + times_t(d_up, w_up))
    weighted = d_normed * scales[:, 1]
    gain_two = jnp.sum(d_normed * middle * scale_two, axis=0)
    d_middle = (
        cotangent.astype(jnp.float32)
        + scale_two * weighted
        - middle * scale_two**3 * jnp.mean(weighted * middle, axis=-1, keepdims=True)
    )
    return (d_middle, (grad_gate, grad_up, grad_down, gain_two))


def backward_attention(record, d_middle, params):
    (
        hidden,
        scale_one,
        normed_one,
        query,
        keys,
        values,
        mixed,
        log_total,
        middle,
        scale_two,
        normed_two,
        gate,
        upward,
        activated,
    ) = record
    scales, w_query, key_weight, value_weight, w_out, w_gate, w_up, down_weight = params
    length = hidden.shape[0]
    groups = keys.shape[1]
    d_mid_low = d_middle.astype(jnp.bfloat16)
    grad_out = over_rows(d_mid_low, mixed)
    d_mixed = jnp.dot(d_mid_low, w_out, preferred_element_type=jnp.float32).astype(jnp.bfloat16)
    d_heads = d_mixed.reshape(length, groups, -1, HEAD_SIZE)
    scores, causal = score_table(query, keys)
    probs = jnp.where(causal, jnp.exp(scores - log_total[..., None]), 0.0)
    d_probs = jnp.einsum("qgrd,kgd->grqk", d_heads, values, preferred_element_type=jnp.float32)
    d_values = jnp.einsum(
        "grqk,qgrd->kgd", probs.astype(jnp.bfloat16), d_heads, preferred_element_type=jnp.float32
    )
    delta = jnp.sum(
        d_heads.astype(jnp.float32)
        * mixed.reshape(length, groups, -1, HEAD_SIZE).astype(jnp.float32),
        axis=-1,
    )
    d_scores = (
        probs * (d_probs - jnp.transpose(delta, (1, 2, 0))[..., None]) * HEAD_SIZE ** (-0.5)
    ).astype(jnp.bfloat16)
    cosine, sine = rope_tables(length, HEAD_SIZE)
    d_query = (
        rotate_back(
            jnp.einsum(
                "grqk,kgd->qgrd", d_scores, keys, preferred_element_type=jnp.float32
            ).reshape(length, -1, HEAD_SIZE),
            cosine,
            sine,
        )
        .astype(jnp.bfloat16)
        .reshape(length, -1)
    )
    d_keys = (
        rotate_back(
            jnp.einsum("grqk,qgrd->kgd", d_scores, query, preferred_element_type=jnp.float32),
            cosine,
            sine,
        )
        .astype(jnp.bfloat16)
        .reshape(length, -1)
    )
    d_vals = d_values.astype(jnp.bfloat16).reshape(length, -1)
    grad_query = over_rows(normed_one, d_query)
    grad_key = over_rows(normed_one, d_keys)
    value_weight_gradient = over_rows(normed_one, d_vals)
    d_first = inputs_total(
        times_t(d_query, w_query) + times_t(d_keys, key_weight) + times_t(d_vals, value_weight)
    )
    weighted_one = d_first * scales[:, 0]
    wide = hidden.astype(jnp.float32)
    gain_one = jnp.sum(d_first * wide * scale_one, axis=0)
    d_hidden = (
        d_middle
        + scale_one * weighted_one
        - wide * scale_one**3 * jnp.mean(weighted_one * wide, axis=-1, keepdims=True)
    ).astype(jnp.bfloat16)
    return (d_hidden, (grad_query, grad_key, value_weight_gradient, grad_out, gain_one))


def body(
    inputs,
    cotangents,
    norm_scales,
    w_query,
    key_weight,
    value_weight,
    w_out,
    w_gate,
    w_up,
    down_weight,
):
    params = (
        norm_scales[0],
        w_query[0],
        key_weight[0],
        value_weight[0],
        w_out[0],
        w_gate[0],
        w_up[0],
        down_weight[0],
    )
    section_index = lax.axis_index("pipe")
    is_first = section_index == 0
    micros = inputs.shape[0]
    length = inputs.shape[2]
    width = inputs.shape[3]
    incoming = jnp.zeros((length, width), jnp.bfloat16)
    saved = []
    results = []
    for step_index in range(micros + 1):
        own_input = inputs[min(step_index, micros - 1), 0]
        record, result = forward_layer(jnp.where(is_first, own_input, incoming), params)
        saved.append(record)
        results.append(result)
        if step_index < micros:
            incoming = passed_along(result, "pipe", 1)
    stacked = jax.tree.map(lambda *entries: jnp.stack(entries), *saved)
    returned = jnp.zeros((length, width), jnp.bfloat16)
    in_grads = []
    for step_index in range(micros + 1):
        micro_index = step_index - 1 + section_index
        weight_mask = jnp.logical_and(micro_index >= 0, micro_index < micros).astype(jnp.float32)
        slot_index = jnp.clip(micro_index + section_index, 0, micros)
        record = jax.tree.map(
            lambda entry: lax.dynamic_index_in_dim(entry, slot_index, 0, keepdims=False), stacked
        )
        cotangent = jnp.where(is_first, returned, cotangents[min(step_index, micros - 1), 0])
        d_middle, ffn_part = backward_feedforward(record, cotangent, params)
        if step_index == 0:
            ffn_sums = jax.tree.map(lambda extra: weight_mask * extra, ffn_part)
        else:
            ffn_sums = jax.tree.map(
                lambda total, extra: total + weight_mask * extra, ffn_sums, ffn_part
            )
        d_hidden, attn_part = backward_attention(record, d_middle, params)
        if step_index == 0:
            attn_sums = jax.tree.map(lambda extra: weight_mask * extra, attn_part)
        else:
            attn_sums = jax.tree.map(
                lambda total, extra: total + weight_mask * extra, attn_sums, attn_part
            )
        in_grads.append(d_hidden)
        if step_index < micros:
            returned = passed_along(d_hidden, "pipe", -1)
    gain_grads = jnp.stack([attn_sums[4], ffn_sums[3]], axis=1)[None]
    shards = (
        lax.psum_scatter(
            attn_sums[0][None].astype(jnp.bfloat16), "dp", scatter_dimension=1, tiled=True
        ).astype(jnp.float32),
        lax.psum_scatter(
            attn_sums[1][None].astype(jnp.bfloat16), "dp", scatter_dimension=1, tiled=True
        ).astype(jnp.float32),
        lax.psum_scatter(
            attn_sums[2][None].astype(jnp.bfloat16), "dp", scatter_dimension=1, tiled=True
        ).astype(jnp.float32),
        lax.psum_scatter(
            attn_sums[3][None].astype(jnp.bfloat16), "dp", scatter_dimension=1, tiled=True
        ).astype(jnp.float32),
        lax.psum_scatter(
            ffn_sums[0][None].astype(jnp.bfloat16), "dp", scatter_dimension=1, tiled=True
        ).astype(jnp.float32),
        lax.psum_scatter(
            ffn_sums[1][None].astype(jnp.bfloat16), "dp", scatter_dimension=1, tiled=True
        ).astype(jnp.float32),
        lax.psum_scatter(
            ffn_sums[2][None].astype(jnp.bfloat16), "dp", scatter_dimension=1, tiled=True
        ).astype(jnp.float32),
        lax.psum_scatter(
            gain_grads.astype(jnp.bfloat16), "dp", scatter_dimension=1, tiled=True
        ).astype(jnp.float32),
    )
    (
        grad_query,
        grad_key,
        value_weight_gradient,
        grad_out,
        grad_gate,
        grad_up,
        grad_down,
        grad_scales,
    ) = shards
    section_out = lax.dynamic_slice_in_dim(jnp.stack(results), section_index, micros, 0).reshape(
        1, micros, 1, length, width
    )
    section_in_grad = lax.dynamic_slice_in_dim(
        jnp.stack(in_grads), 1 - section_index, micros, 0
    ).reshape(1, micros, 1, length, width)
    return (
        section_out,
        section_in_grad,
        grad_scales,
        grad_query,
        grad_key,
        value_weight_gradient,
        grad_out,
        grad_gate,
        grad_up,
        grad_down,
    )


def solution(mesh):
    placed = (
        P(None, "dp", None, None),
        P(None, "dp", None, None),
        P("pipe", None, None),
        P("pipe", None, "tensor"),
        P("pipe", None, "tensor"),
        P("pipe", None, "tensor"),
        P("pipe", None, "tensor"),
        P("pipe", None, "tensor"),
        P("pipe", None, "tensor"),
        P("pipe", None, "tensor"),
    )
    return jax.shard_map(
        body,
        mesh=mesh,
        in_specs=placed,
        out_specs=(
            P("pipe", None, "dp", None, None),
            P("pipe", None, "dp", None, None),
            P("pipe", "dp", None),
            P("pipe", "dp", "tensor"),
            P("pipe", "dp", "tensor"),
            P("pipe", "dp", "tensor"),
            P("pipe", "dp", "tensor"),
            P("pipe", "dp", "tensor"),
            P("pipe", "dp", "tensor"),
            P("pipe", "dp", "tensor"),
        ),
        check_vma=False,
    )
```

profile of v0, /device:TPU:0, one launch (start us, length us, event | category | flops | bytes accessed | tf_op | source)
XLA Modules:
  0.0 1268.2 jit_solution(18007858066272877327)
XLA Ops:
  32.4 21.8 %all-reduce.13.cloned.1.call-done = bf16[256,1536]{1,0:T(8,128)(2,1)} async-done(((bf16[256,1536]{1,0:T(8,128)(2,1)}), bf16[256,1536]{1,0:T(8,128)(2,1)}) %all-reduce.13.cloned.1.call-update) | async-done | bytes 786448 | tf_op jit(solution)/shard_map/psum | solution.py:54
  71.2 20.3 %all-reduce.15.cloned.1.call-done = bf16[256,1536]{1,0:T(8,128)(2,1)} async-done(((bf16[256,1536]{1,0:T(8,128)(2,1)}), bf16[256,1536]{1,0:T(8,128)(2,1)}) %all-reduce.15.cloned.1.call-update) | async-done | bytes 786448 | tf_op jit(solution)/shard_map/psum | solution.py:54
  97.9 16.7 %collective-permute-done = bf16[256,1536]{1,0:T(8,128)(2,1)S(1)} collective-permute-done((bf16[256,1536]{1,0:T(8,128)(2,1)S(1)}, bf16[256,1536]{1,0:T(8,128)(2,1)S(1)}, u32[]{:S(2)}, u32[]{:S(2)}) %collective-permute-start) | collective-permute-done | bytes 786464 | tf_op jit(solution)/shard_map/ppermute | solution.py:16
  128.9 21.0 %all-reduce.17.cloned.1.call-done = bf16[256,1536]{1,0:T(8,128)(2,1)} async-done(((bf16[256,1536]{1,0:T(8,128)(2,1)}), bf16[256,1536]{1,0:T(8,128)(2,1)}) %all-reduce.17.cloned.1.call-update) | async-done | bytes 786448 | tf_op jit(solution)/shard_map/psum | solution.py:54
  165.5 20.3 %all-reduce.19.cloned.1.call-done = bf16[256,1536]{1,0:T(8,128)(2,1)} async-done(((bf16[256,1536]{1,0:T(8,128)(2,1)}), bf16[256,1536]{1,0:T(8,128)(2,1)}) %all-reduce.19.cloned.1.call-update) | async-done | bytes 786448 | tf_op jit(solution)/shard_map/psum | solution.py:54
  193.4 16.6 %collective-permute-done.1 = bf16[256,1536]{1,0:T(8,128)(2,1)} collective-permute-done((bf16[256,1536]{1,0:T(8,128)(2,1)}, bf16[256,1536]{1,0:T(8,128)(2,1)}, u32[]{:S(2)}, u32[]{:S(2)}) %collective-permute-start.1) | collective-permute-done | bytes 786464 | tf_op jit(solution)/shard_map/ppermute | solution.py:16
  235.1 11.6 all-reduce.21.cloned.1.call-done
  263.1 7.5 fusion.132
  283.9 14.7 %all-reduce.23.cloned.1.call-done = bf16[256,1536]{1,0:T(8,128)(2,1)} async-done(((bf16[256,1536]{1,0:T(8,128)(2,1)}), bf16[256,1536]{1,0:T(8,128)(2,1)}) %all-reduce.23.cloned.1.call-update) | async-done | bytes 786448 | tf_op jit(solution)/shard_map/psum | solution.py:58
  324.6 16.6 %all-reduce.25.cloned.1.call-done = bf16[256,1536]{1,0:T(8,128)(2,1)} async-done(((bf16[256,1536]{1,0:T(8,128)(2,1)}), bf16[256,1536]{1,0:T(8,128)(2,1)}) %all-reduce.25.cloned.1.call-update) | async-done | bytes 786448 | tf_op jit(solution)/shard_map/psum | solution.py:58
  347.8 20.0 %collective-permute-done.2 = bf16[256,1536]{1,0:T(8,128)(2,1)S(1)} collective-permute-done((bf16[256,1536]{1,0:T(8,128)(2,1)S(1)}, bf16[256,1536]{1,0:T(8,128)(2,1)S(1)}, u32[]{:S(2)}, u32[]{:S(2)}) %collective-permute-start.2) | collective-permute-done | bytes 786464 | tf_op jit(solution)/shard_map/ppermute | solution.py:16
  367.9 6.6 fusion.118
  382.6 16.1 %all-reduce.27.cloned.1.call-done = bf16[256,1536]{1,0:T(8,128)(2,1)} async-done(((bf16[256,1536]{1,0:T(8,128)(2,1)}), bf16[256,1536]{1,0:T(8,128)(2,1)}) %all-reduce.27.cloned.1.call-update) | async-done | bytes 786448 | tf_op jit(solution)/shard_map/psum | solution.py:58
  422.3 18.9 %all-reduce.29.cloned.1.call-done = bf16[256,1536]{1,0:T(8,128)(2,1)} async-done(((bf16[256,1536]{1,0:T(8,128)(2,1)}), bf16[256,1536]{1,0:T(8,128)(2,1)}) %all-reduce.29.cloned.1.call-update) | async-done | bytes 786448 | tf_op jit(solution)/shard_map/psum | solution.py:58
  450.3 17.2 %collective-permute-done.3 = bf16[256,1536]{1,0:T(8,128)(2,1)S(1)} collective-permute-done((bf16[256,1536]{1,0:T(8,128)(2,1)S(1)}, bf16[256,1536]{1,0:T(8,128)(2,1)S(1)}, u32[]{:S(2)}, u32[]{:S(2)}) %collective-permute-start.3) | collective-permute-done | bytes 786464 | tf_op jit(solution)/shard_map/ppermute | solution.py:16
  467.6 6.6 fusion.104
  492.5 12.1 all-reduce.31.cloned.1.call-done
  529.3 19.4 %all-reduce.33.cloned.1.call-done = (bf16[256,1536]{1,0:T(8,128)(2,1)}, bf16[256,1536]{1,0:T(8,128)(2,1)}) async-done(((bf16[256,1536]{1,0:T(8,128)(2,1)}, bf16[256,1536]{1,0:T(8,128)(2,1)}), (bf16[256,1536]{1,0:T(8,128)(2,1)}, bf16[256,1536]{1,0:T(8,128)(2,1)})) %all-reduce.33.cloned.1.call-update) | async-done | bytes 1572880 | tf_op jit(solution)/shard_map/psum | solution.py:54
  590.9 6.5 fusion.296
  597.4 12.5 fusion
  611.1 7.7 fusion.298
  618.8 6.5 fusion.294
  625.3 12.6 fusion.1
  647.6 6.5 fusion.256
  654.2 12.6 fusion.2
  674.1 11.2 reduce-scatter.13.cloned.1.call-done
  686.9 65.5 %reduce-scatter.15.cloned.1.call-done = bf16[1,192,384]{2,1,0:T(8,128)(2,1)} async-done(((bf16[1,1536,384]{2,1,0:T(8,128)(2,1)}), bf16[1,192,384]{2,1,0:T(8,128)(2,1)}) %reduce-scatter.15.cloned.1.call-update) | async-done | bytes 147472 | tf_op jit(solution)/shard_map/reduce_scatter | solution.py:324
  754.1 70.3 %reduce-scatter.17.cloned.1.call-done = bf16[1,192,768]{2,1,0:T(8,128)(2,1)} async-done(((bf16[1,1536,768]{2,1,0:T(8,128)(2,1)}), bf16[1,192,768]{2,1,0:T(8,128)(2,1)}) %reduce-scatter.17.cloned.1.call-update) | async-done | bytes 294928 | tf_op jit(solution)/shard_map/reduce_scatter | solution.py:327
  826.2 70.4 %reduce-scatter.11.cloned.1.call-done = bf16[1,192,768]{2,1,0:T(8,128)(2,1)} async-done(((bf16[1,1536,768]{2,1,0:T(8,128)(2,1)}), bf16[1,192,768]{2,1,0:T(8,128)(2,1)}) %reduce-scatter.11.cloned.1.call-update) | async-done | bytes 294928 | tf_op jit(solution)/shard_map/reduce_scatter | solution.py:318
  898.4 118.9 %reduce-scatter.19.cloned.1.call-done = bf16[1,192,2048]{2,1,0:T(8,128)(2,1)} async-done(((bf16[1,1536,2048]{2,1,0:T(8,128)(2,1)}), bf16[1,192,2048]{2,1,0:T(8,128)(2,1)}) %reduce-scatter.19.cloned.1.call-update) | async-done | bytes 786448 | tf_op jit(solution)/shard_map/reduce_scatter | solution.py:330
  1019.8 118.3 %reduce-scatter.21.cloned.1.call-done = bf16[1,192,2048]{2,1,0:T(8,128)(2,1)} async-done(((bf16[1,1536,2048]{2,1,0:T(8,128)(2,1)}), bf16[1,192,2048]{2,1,0:T(8,128)(2,1)}) %reduce-scatter.21.cloned.1.call-update) | async-done | bytes 786448 | tf_op jit(solution)/shard_map/reduce_scatter | solution.py:333
  1140.5 118.4 %reduce-scatter.23.cloned.1.call-done = bf16[1,192,2048]{2,1,0:T(8,128)(2,1)} async-done(((bf16[1,1536,2048]{2,1,0:T(8,128)(2,1)}), bf16[1,192,2048]{2,1,0:T(8,128)(2,1)}) %reduce-scatter.23.cloned.1.call-update) | async-done | bytes 786448 | tf_op jit(solution)/shard_map/reduce_scatter | solution.py:336
  (618 shorter events, 329.9 us)
Async XLA Ops:
  7.2 23.4 %copy-start = (bf16[1,1536,768]{2,1,0:T(8,128)(2,1)S(1)}, bf16[1,1536,768]{2,1,0:T(8,128)(2,1)}, u32[]{:S(2)}) copy-start(bf16[1,1536,768]{2,1,0:T(8,128)(2,1)} %param.16) | copy-start | bytes 7077892
  7.2 47.0 %all-reduce.13.cloned.1.call-start = ((), (), s32[]{:S(2)}) async-start(), calls=%async_computation.8 | async-start | bytes 1572864 | tf_op jit(solution)/shard_map/psum | solution.py:54
  32.3 59.2 %all-reduce.15.cloned.1.call-start = ((), (), s32[]{:S(2)}) async-start(), calls=%async_computation.9 | async-start | bytes 1572864 | tf_op jit(solution)/shard_map/psum | solution.py:54
  71.2 78.7 %all-reduce.17.cloned.1.call-start = ((), (), s32[]{:S(2)}) async-start(), calls=%async_computation.10 | async-start | bytes 1572864 | tf_op jit(solution)/shard_map/psum | solution.py:54
  91.5 23.4 %copy-start.24 = (bf16[1,1536,384]{2,1,0:T(8,128)(2,1)S(1)}, bf16[1,1536,384]{2,1,0:T(8,128)(2,1)}, u32[]{:S(2)}) copy-start(bf16[1,1536,384]{2,1,0:T(8,128)(2,1)} %param.15) | copy-start | bytes 3538948
  93.4 21.1 %collective-permute-start = (bf16[256,1536]{1,0:T(8,128)(2,1)S(1)}, bf16[256,1536]{1,0:T(8,128)(2,1)S(1)}, u32[]{:S(2)}, u32[]{:S(2)}) collective-permute-start(bf16[256,1536]{1,0:T(8,128)(2,1)S(1)} %add_convert_fusion.7), channel_id=1, source_target_pairs={{0,16},{1,17},{2,18},{3,19},{4,20},{5,21},{6,22},{7,23},{8,24},{9,... | collective-permute-start | bytes 2359304 | tf_op jit(solution)/shard_map/ppermute | solution.py:16
  114.9 70.9 %copy-start.18 = (bf16[256,1536]{1,0:T(8,128)(2,1)}, bf16[256,1536]{1,0:T(8,128)(2,1)S(1)}, u32[]{:S(2)}) copy-start(bf16[256,1536]{1,0:T(8,128)(2,1)S(1)} %get-tuple-element.29) | copy-start | bytes 2359300
  128.8 57.0 %all-reduce.19.cloned.1.call-start = ((), (), s32[]{:S(2)}) async-start(), calls=%async_computation.11 | async-start | bytes 1572864 | tf_op jit(solution)/shard_map/psum | solution.py:54
  165.5 81.2 %all-reduce.21.cloned.1.call-start = ((), (), s32[]{:S(2)}) async-start(), calls=%async_computation.12 | async-start | bytes 1572864 | tf_op jit(solution)/shard_map/psum | solution.py:54
  188.8 21.2 %collective-permute-start.1 = (bf16[256,1536]{1,0:T(8,128)(2,1)}, bf16[256,1536]{1,0:T(8,128)(2,1)}, u32[]{:S(2)}, u32[]{:S(2)}) collective-permute-start(bf16[256,1536]{1,0:T(8,128)(2,1)} %get-tuple-element.46), channel_id=1, source_target_pairs={{0,16},{1,17},{2,18},{3,19},{4,20},{5,21},{6,22},{7,23},{8,24},{9,... | collective-permute-start | bytes 2359304 | tf_op jit(solution)/shard_map/ppermute | solution.py:16
  225.4 73.2 %all-reduce.23.cloned.1.call-start = ((), (), s32[]{:S(2)}) async-start(), calls=%async_computation.13 | async-start | bytes 1572864 | tf_op jit(solution)/shard_map/psum | solution.py:58
  278.2 63.0 %all-reduce.25.cloned.1.call-start = ((), (), s32[]{:S(2)}) async-start(), calls=%async_computation.14 | async-start | bytes 1572864 | tf_op jit(solution)/shard_map/psum | solution.py:58
  320.9 77.8 %all-reduce.27.cloned.1.call-start = ((), (), s32[]{:S(2)}) async-start(), calls=%async_computation.15 | async-start | bytes 1572864 | tf_op jit(solution)/shard_map/psum | solution.py:58
  343.8 24.1 %copy-start.43 = (bf16[2,1,256,1536]{3,2,1,0:T(8,128)(2,1)S(1)}, bf16[2,1,256,1536]{3,2,1,0:T(8,128)(2,1)}, u32[]{:S(2)}) copy-start(bf16[2,1,256,1536]{3,2,1,0:T(8,128)(2,1)} %param.11) | copy-start | bytes 4718596
  343.8 30.8 %slice-start.6 = ((s8[6291456]{0:T(1024)(128)(4,1)}), s8[4194304]{0:T(1024)(128)(4,1)S(1)}, s32[]{:S(2)}) async-start(s8[6291456]{0:T(1024)(128)(4,1)} %bitcast.922), calls=%async_computation.33 | async-start | bytes 8388608
  343.8 32.8 %slice-start.8 = ((s8[6291456]{0:T(1024)(128)(4,1)}), s8[4194304]{0:T(1024)(128)(4,1)S(1)}, s32[]{:S(2)}) async-start(s8[6291456]{0:T(1024)(128)(4,1)} %bitcast.924), calls=%async_computation.35 | async-start | bytes 8388608
  345.8 22.0 %collective-permute-start.2 = (bf16[256,1536]{1,0:T(8,128)(2,1)S(1)}, bf16[256,1536]{1,0:T(8,128)(2,1)S(1)}, u32[]{:S(2)}, u32[]{:S(2)}) collective-permute-start(bf16[256,1536]{1,0:T(8,128)(2,1)S(1)} %fusion.176), channel_id=1, source_target_pairs={{16,0},{17,1},{18,2},{19,3},{20,4},{21,5},{22,6},{23,7},{24,8},{25... | collective-permute-start | bytes 2359304 | tf_op jit(solution)/shard_map/ppermute | solution.py:16
  379.4 61.9 %all-reduce.29.cloned.1.call-start = ((), (), s32[]{:S(2)}) async-start(), calls=%async_computation.16 | async-start | bytes 1572864 | tf_op jit(solution)/shard_map/psum | solution.py:58
  420.9 83.7 %all-reduce.31.cloned.1.call-start = ((), (), s32[]{:S(2)}) async-start(), calls=%async_computation.17 | async-start | bytes 1572864 | tf_op jit(solution)/shard_map/psum | solution.py:58
  445.8 21.7 %collective-permute-start.3 = (bf16[256,1536]{1,0:T(8,128)(2,1)S(1)}, bf16[256,1536]{1,0:T(8,128)(2,1)S(1)}, u32[]{:S(2)}, u32[]{:S(2)}) collective-permute-start(bf16[256,1536]{1,0:T(8,128)(2,1)S(1)} %fusion.170), channel_id=1, source_target_pairs={{16,0},{17,1},{18,2},{19,3},{20,4},{21,5},{22,6},{23,7},{24,8},{25... | collective-permute-start | bytes 2359304 | tf_op jit(solution)/shard_map/ppermute | solution.py:16
  485.2 63.5 %all-reduce.33.cloned.1.call-start = ((), (), s32[]{:S(2)}) async-start(), calls=%async_computation.26 | async-start | bytes 3145728 | tf_op jit(solution)/shard_map/psum | solution.py:54
  526.9 23.7 %copy-start.146 = (f32[1536]{0:T(1024)S(1)}, f32[1536]{0:T(1024)}, u32[]{:S(2)}) copy-start(f32[1536]{0:T(1024)} %get-tuple-element.16) | copy-start | bytes 18436
  526.9 23.7 %copy-start.148 = (f32[1536]{0:T(1024)S(1)}, f32[1536]{0:T(1024)}, u32[]{:S(2)}) copy-start(f32[1536]{0:T(1024)} %get-tuple-element.18) | copy-start | bytes 18436
  526.9 145.7 %reduce-scatter.25.cloned.1.call-start = ((), (), s32[]{:S(2)}) async-start(), calls=%async_computation.25 | async-start | bytes 442368
  529.3 25.2 %copy-start.158 = (f32[256]{0:T(256)S(1)}, f32[256]{0:T(256)}, u32[]{:S(2)}) copy-start(f32[256]{0:T(256)} %copy-done.156) | copy-start | bytes 3076
  554.4 130.9 %reduce-scatter.13.cloned.1.call-start = ((), (), s32[]{:S(2)}) async-start(), calls=%async_computation.19 | async-start | bytes 1327104 | tf_op jit(solution)/shard_map/reduce_scatter | solution.py:321
  563.3 189.2 %reduce-scatter.15.cloned.1.call-start = ((), (), s32[]{:S(2)}) async-start(), calls=%async_computation.20 | async-start | bytes 1327104 | tf_op jit(solution)/shard_map/reduce_scatter | solution.py:324
  568.1 256.3 %reduce-scatter.17.cloned.1.call-start = ((), (), s32[]{:S(2)}) async-start(), calls=%async_computation.21 | async-start | bytes 2654208 | tf_op jit(solution)/shard_map/reduce_scatter | solution.py:327
  574.8 321.7 %reduce-scatter.11.cloned.1.call-start = ((), (), s32[]{:S(2)}) async-start(), calls=%async_computation.18 | async-start | bytes 2654208 | tf_op jit(solution)/shard_map/reduce_scatter | solution.py:318
  581.6 435.7 %reduce-scatter.19.cloned.1.call-start = ((), (), s32[]{:S(2)}) async-start(), calls=%async_computation.22 | async-start | bytes 7077888 | tf_op jit(solution)/shard_map/reduce_scatter | solution.py:330
  609.9 528.2 %reduce-scatter.21.cloned.1.call-start = ((), (), s32[]{:S(2)}) async-start(), calls=%async_computation.23 | async-start | bytes 7077888 | tf_op jit(solution)/shard_map/reduce_scatter | solution.py:333
  637.9 621.1 %reduce-scatter.23.cloned.1.call-start = ((), (), s32[]{:S(2)}) async-start(), calls=%async_computation.24 | async-start | bytes 7077888 | tf_op jit(solution)/shard_map/reduce_scatter | solution.py:336
  (174 other events, 665.5 us)
Sparse Core Ops, SparseCore 0:
  32.5 21.6 all-reduce.12
  71.3 20.1 all-reduce.14
  128.9 20.8 all-reduce.16
  165.6 20.1 all-reduce.18
  225.5 21.1 all-reduce.20
  278.4 20.1 all-reduce.22
  321.0 20.1 all-reduce.24
  379.5 19.1 all-reduce.26
  421.0 20.1 all-reduce.28
  485.3 19.2 all-reduce.30
  527.0 21.6 all-reduce.32
  554.5 63.3 reduce-scatter.24
  621.4 63.8 reduce-scatter.12
  688.5 63.8 reduce-scatter.14
  755.8 68.5 reduce-scatter.16
  827.7 68.8 reduce-scatter.10
  900.0 117.2 reduce-scatter.18
  1020.8 117.2 reduce-scatter.20
  1141.7 117.2 reduce-scatter.22
where the time goes:
time: 1280 us; the launch traced here: 1270 us
  waiting for transfers between devices  837 us (65%)
  matrix products  240 us (19%)
  other arithmetic  105 us (8%)
  local copies, waits for them, and re-layouts  55.1 us (4%)
  between operations  16.5 us (1%)
  starting transfers between devices  14.8 us (1%)
    reduce_scatter x1, waiting for transfers between devices, body(): lax.psum_scatter(ffn_sums[0][None].astype(jnp.bfloat16), 'dp', scatter_di...  119 us
    reduce_scatter x1, waiting for transfers between devices, body(): lax.psum_scatter(ffn_sums[2][None].astype(jnp.bfloat16), 'dp', scatter_di...  118 us
    reduce_scatter x1, waiting for transfers between devices, body(): lax.psum_scatter(ffn_sums[1][None].astype(jnp.bfloat16), 'dp', scatter_di...  118 us
    psum x6, waiting for transfers between devices, heads_total(): lax.psum(partial_value.astype(jnp.bfloat16), 'tensor').astype(jnp.float32)  114 us
    dot_general x21, matrix products, over_rows(): lax.dot_general(left, right, (((0,), (0,)), ((), ())), preferred_element_...  96.3 us
    psum x5, waiting for transfers between devices, inputs_total(): lax.psum(partial_value.astype(jnp.bfloat16), 'tensor').astype(jnp.float32)  78.4 us
    ppermute x4, waiting for transfers between devices, passed_along(): return lax.ppermute(value, axis, pairs)  70.5 us
    reduce_scatter x1, waiting for transfers between devices, body(): lax.psum_scatter(attn_sums[0][None].astype(jnp.bfloat16), 'dp', scatter_d...  70.4 us
  transfers between devices with their start and end apart: 23, of which 22 were waited for; matrix products, arithmetic and copies ran while one was open for 12% of the time, Pallas kernels for 0%

commit v1 on v0

--- a/solution.py
+++ b/solution.py
@@ -1,6 +1,8 @@
 import jax
 import jax.numpy as jnp
 from jax import lax
+from jax.experimental import pallas as pl
+from jax.experimental.pallas import tpu as pltpu
 from jax.sharding import PartitionSpec as P
 
 HEAD_SIZE = 96
@@ -51,11 +53,185 @@
 
 
 def heads_total(partial_value):
-    return lax.psum(partial_value.astype(jnp.bfloat16), "tensor").astype(jnp.float32)
-
-
-def inputs_total(partial_value):
-    return lax.psum(partial_value.astype(jnp.bfloat16), "tensor").astype(jnp.float32)
+    low = partial_value.astype(jnp.bfloat16)
+    total = low.astype(jnp.float32)
+    peers = lax.axis_size("tensor")
+    for by in range(1, peers):
+        other = lax.ppermute(low, "tensor", [(i, (i + by) % peers) for i in range(peers)])
+        total = total + other.astype(jnp.float32)
+    return total
+
+
+inputs_total = heads_total
+
+
+def bit_orders(bits):
+    plain = list(range(bits))
+    if bits < 2:
+        return [plain]
+    swapped = [1, 0] + plain[2:]
+    return [plain, plain, plain, swapped]
+
+
+def halving_kernel(widths, blocks, bits, axis, *refs):
+    count = len(widths)
+    grads, outs = refs[:count], refs[count : 2 * count]
+    rest = refs[2 * count :]
+    local, got = rest[:count], rest[count : count + count * bits]
+    load_sem, send_sem, recv_sem = rest[count + count * bits :]
+    me = lax.axis_index(axis)
+    own = [lax.rem(lax.div(me, 2**bit), 2) for bit in range(bits)]
+    flip = [me + (1 - 2 * own[bit]) * 2**bit for bit in range(bits)]
+    barrier = pltpu.get_barrier_semaphore()
+    for bit in range(bits):
+        pl.semaphore_signal(
+            barrier, inc=1, device_id={axis: flip[bit]}, device_id_type=pl.DeviceIdType.MESH
+        )
+    pl.semaphore_wait(barrier, bits)
+    orders = bit_orders(bits)
+    chunks = []
+    for which, width in enumerate(widths):
+        for at in range(grads[which].shape[-1] // width):
+            chunks.append((which, at))
+    plans = [orders[number % len(orders)] for number in range(len(chunks))]
+
+    def place(fixed, free):
+        return tuple(fixed[bit] if bit in fixed else slice(None) for bit in reversed(range(bits)))
+
+    loads, sends = [], {}
+    for number, (which, at) in enumerate(chunks):
+        first = plans[number][0]
+        width = widths[which]
+        columns = pl.ds(at * width, width)
+        theirs = place({first: 1 - own[first]}, None)
+        mine = place({first: own[first]}, None)
+        send = pltpu.make_async_remote_copy(
+            src_ref=grads[which].at[theirs + (slice(None), columns)],
+            dst_ref=got[which * bits].at[at],
+            send_sem=send_sem.at[number, 0],
+            recv_sem=recv_sem.at[number, 0],
+            device_id={axis: flip[first]},
+            device_id_type=pl.DeviceIdType.MESH,
+        )
+        send.start()
+        sends[number, 0] = send
+        load = pltpu.make_async_copy(
+            grads[which].at[mine + (slice(None), columns)], local[which].at[at], load_sem.at[number]
+        )
+        load.start()
+        loads.append(load)
+
+    def step(number, level):
+        which, at = chunks[number]
+        order = plans[number]
+        width = widths[which]
+        block = blocks[which]
+        if level == 0:
+            loads[number].wait()
+        sends[number, level].wait_recv()
+        done = order[: level + 1]
+        left = [bit for bit in reversed(range(bits)) if bit not in done]
+        before = [bit for bit in reversed(range(bits)) if bit not in order[:level]]
+        received = got[which * bits + level].at[at]
+        kept_first = order[0]
+        axes = [bit for bit in reversed(range(bits)) if bit != kept_first]
+        rows = block if block % 64 else 64
+
+        def view(fixed):
+            return tuple(fixed[bit] for bit in axes)
+
+        for combo in range(2 ** len(left)):
+            fixed = {bit: (combo >> index) & 1 for index, bit in enumerate(left)}
+            for bit in done:
+                fixed[bit] = own[bit]
+            spot = view(fixed)
+            from_spot = tuple(fixed[bit] for bit in left)
+
+            def add(piece, _):
+                where = pl.ds(pl.multiple_of(piece * rows, rows), rows)
+                a = local[which][(at,) + spot + (where, slice(None))].astype(jnp.float32)
+                b = received[from_spot + (where, slice(None))].astype(jnp.float32)
+                if level == bits - 1:
+                    outs[which][where, pl.ds(at * width, width)] = (a + b).astype(jnp.bfloat16)
+                else:
+                    local[which][(at,) + spot + (where, slice(None))] = (a + b).astype(jnp.bfloat16)
+                return 0
+
+            lax.fori_loop(0, block // rows, add, 0)
+        if level < bits - 1:
+            following = order[level + 1]
+            source = []
+            for bit in axes:
+                if bit in done:
+                    source.append(own[bit])
+                elif bit == following:
+                    source.append(1 - own[bit])
+                else:
+                    source.append(slice(None))
+            send = pltpu.make_async_remote_copy(
+                src_ref=local[which].at[(at,) + tuple(source)],
+                dst_ref=got[which * bits + level + 1].at[at],
+                send_sem=send_sem.at[number, level + 1],
+                recv_sem=recv_sem.at[number, level + 1],
+                device_id={axis: flip[following]},
+                device_id_type=pl.DeviceIdType.MESH,
+            )
+            send.start()
+            sends[number, level + 1] = send
+
+    for tick in range(len(chunks) + bits - 1):
+        for level in range(bits):
+            number = tick - level
+            if 0 <= number < len(chunks):
+                step(number, level)
+    for send in sends.values():
+        send.wait_send()
+
+
+def scattered(grads, axis):
+    peers = lax.axis_size(axis)
+    bits = peers.bit_length() - 1
+    blocks = [grad.shape[0] // peers for grad in grads]
+    widths = []
+    for grad in grads:
+        columns = grad.shape[1]
+        widths.append(next(w for w in (256, 384, 128) if columns % w == 0))
+    shaped = [
+        grad.reshape((2,) * bits + (block, grad.shape[1])) for grad, block in zip(grads, blocks)
+    ]
+    pieces = [grad.shape[1] // width for grad, width in zip(grads, widths)]
+    scratch = [
+        pltpu.VMEM((piece,) + (2,) * (bits - 1) + (block, width), jnp.bfloat16)
+        for piece, block, width in zip(pieces, blocks, widths)
+    ]
+    for piece, block, width in zip(pieces, blocks, widths):
+        for level in range(bits):
+            scratch.append(
+                pltpu.VMEM((piece,) + (2,) * (bits - 1 - level) + (block, width), jnp.bfloat16)
+            )
+    total = sum(pieces)
+    scratch += [
+        pltpu.SemaphoreType.DMA((total,)),
+        pltpu.SemaphoreType.DMA((total, bits)),
+        pltpu.SemaphoreType.DMA((total, bits)),
+    ]
+
+    def kernel(*refs):
+        halving_kernel(widths, blocks, bits, axis, *refs)
+
+    return pl.pallas_call(
+        kernel,
+        out_shape=[
+            jax.ShapeDtypeStruct((block, grad.shape[1]), jnp.bfloat16)
+            for grad, block in zip(grads, blocks)
+        ],
+        in_specs=[pl.BlockSpec(memory_space=pl.ANY)] * len(grads),
+        out_specs=[pl.BlockSpec(memory_space=pltpu.VMEM)] * len(grads),
+        scratch_shapes=scratch,
+        compiler_params=pltpu.CompilerParams(
+            collective_id=0, has_side_effects=True, vmem_limit_bytes=60 * 2**20
+        ),
+    )(*shaped)
 
 
 def norm_rows(values, gain):
@@ -153,13 +329,10 @@
         activated,
     ) = record
     scales, w_query, key_weight, value_weight, w_out, w_gate, w_up, down_weight = params
-    grad_down = over_rows(cotangent, activated)
     d_act = jnp.dot(cotangent, down_weight, preferred_element_type=jnp.float32)
     sig = jax.nn.sigmoid(gate)
     d_gate = (d_act * upward * sig * (1.0 + gate * (1.0 - sig))).astype(jnp.bfloat16)
     d_up = (d_act * gate * sig).astype(jnp.bfloat16)
-    grad_gate = over_rows(normed_two, d_gate)
-    grad_up = over_rows(normed_two, d_up)
     d_normed = inputs_total(times_t(d_gate, w_gate) + times_t(d_up, w_up))
     weighted = d_normed * scales[:, 1]
     gain_two = jnp.sum(d_normed * middle * scale_two, axis=0)
@@ -168,7 +341,7 @@
         + scale_two * weighted
         - middle * scale_two**3 * jnp.mean(weighted * middle, axis=-1, keepdims=True)
     )
-    return (d_middle, (grad_gate, grad_up, grad_down, gain_two))
+    return (d_middle, (normed_two, d_gate, d_up, cotangent, activated, gain_two))
 
 
 def backward_attention(record, d_middle, params):
@@ -192,7 +365,6 @@
     length = hidden.shape[0]
     groups = keys.shape[1]
     d_mid_low = d_middle.astype(jnp.bfloat16)
-    grad_out = over_rows(d_mid_low, mixed)
     d_mixed = jnp.dot(d_mid_low, w_out, preferred_element_type=jnp.float32).astype(jnp.bfloat16)
     d_heads = d_mixed.reshape(length, groups, -1, HEAD_SIZE)
     scores, causal = score_table(query, keys)
@@ -231,9 +403,6 @@
         .reshape(length, -1)
     )
     d_vals = d_values.astype(jnp.bfloat16).reshape(length, -1)
-    grad_query = over_rows(normed_one, d_query)
-    grad_key = over_rows(normed_one, d_keys)
-    value_weight_gradient = over_rows(normed_one, d_vals)
     d_first = inputs_total(
         times_t(d_query, w_query) + times_t(d_keys, key_weight) + times_t(d_vals, value_weight)
     )
@@ -245,7 +414,7 @@
         + scale_one * weighted_one
         - wide * scale_one**3 * jnp.mean(weighted_one * wide, axis=-1, keepdims=True)
     ).astype(jnp.bfloat16)
-    return (d_hidden, (grad_query, grad_key, value_weight_gradient, grad_out, gain_one))
+    return (d_hidden, (normed_one, d_query, d_keys, d_vals, d_mid_low, mixed, gain_one))
 
 
 def body(
@@ -288,58 +457,59 @@
     stacked = jax.tree.map(lambda *entries: jnp.stack(entries), *saved)
     returned = jnp.zeros((length, width), jnp.bfloat16)
     in_grads = []
+    parts = []
     for step_index in range(micros + 1):
         micro_index = step_index - 1 + section_index
-        weight_mask = jnp.logical_and(micro_index >= 0, micro_index < micros).astype(jnp.float32)
         slot_index = jnp.clip(micro_index + section_index, 0, micros)
         record = jax.tree.map(
             lambda entry: lax.dynamic_index_in_dim(entry, slot_index, 0, keepdims=False), stacked
         )
         cotangent = jnp.where(is_first, returned, cotangents[min(step_index, micros - 1), 0])
         d_middle, ffn_part = backward_feedforward(record, cotangent, params)
-        if step_index == 0:
-            ffn_sums = jax.tree.map(lambda extra: weight_mask * extra, ffn_part)
-        else:
-            ffn_sums = jax.tree.map(
-                lambda total, extra: total + weight_mask * extra, ffn_sums, ffn_part
-            )
         d_hidden, attn_part = backward_attention(record, d_middle, params)
-        if step_index == 0:
-            attn_sums = jax.tree.map(lambda extra: weight_mask * extra, attn_part)
-        else:
-            attn_sums = jax.tree.map(
-                lambda total, extra: total + weight_mask * extra, attn_sums, attn_part
-            )
+        parts.append(ffn_part + attn_part)
         in_grads.append(d_hidden)
         if step_index < micros:
             returned = passed_along(d_hidden, "pipe", -1)
-    gain_grads = jnp.stack([attn_sums[4], ffn_sums[3]], axis=1)[None]
-    shards = (
-        lax.psum_scatter(
-            attn_sums[0][None].astype(jnp.bfloat16), "dp", scatter_dimension=1, tiled=True
-        ).astype(jnp.float32),
-        lax.psum_scatter(
-            attn_sums[1][None].astype(jnp.bfloat16), "dp", scatter_dimension=1, tiled=True
-        ).astype(jnp.float32),
-        lax.psum_scatter(
-            attn_sums[2][None].astype(jnp.bfloat16), "dp", scatter_dimension=1, tiled=True
-        ).astype(jnp.float32),
-        lax.psum_scatter(
-            attn_sums[3][None].astype(jnp.bfloat16), "dp", scatter_dimension=1, tiled=True
-        ).astype(jnp.float32),
-        lax.psum_scatter(
-            ffn_sums[0][None].astype(jnp.bfloat16), "dp", scatter_dimension=1, tiled=True
-        ).astype(jnp.float32),
-        lax.psum_scatter(
-            ffn_sums[1][None].astype(jnp.bfloat16), "dp", scatter_dimension=1, tiled=True
-        ).astype(jnp.float32),
-        lax.psum_scatter(
-            ffn_sums[2][None].astype(jnp.bfloat16), "dp", scatter_dimension=1, tiled=True
-        ).astype(jnp.float32),
-        lax.psum_scatter(
-            gain_grads.astype(jnp.bfloat16), "dp", scatter_dimension=1, tiled=True
-        ).astype(jnp.float32),
-    )
+    kept = jax.tree.map(
+        lambda *entries: lax.dynamic_slice_in_dim(
+            jnp.stack(entries), 1 - section_index, micros, 0
+        ),
+        *parts,
+    )
+    (
+        normed_two,
+        d_gate,
+        d_up,
+        cotangent,
+        activated,
+        gain_two,
+        normed_one,
+        d_query,
+        d_keys,
+        d_vals,
+        d_mid_low,
+        mixed,
+        gain_one,
+    ) = (entry.reshape(-1, entry.shape[-1]) for entry in kept)
+    dp_size = lax.axis_size("dp")
+    gains = jnp.stack([gain_one.sum(axis=0), gain_two.sum(axis=0)], axis=1)
+    gains = gains.astype(jnp.bfloat16).reshape(dp_size, -1)
+    gain_size = gains.shape[1]
+    gains = jnp.pad(gains, ((0, 0), (0, 2048 - gain_size))).reshape(dp_size * 16, 128)
+    grads = [
+        over_rows(normed_one, d_query),
+        over_rows(normed_one, d_keys),
+        over_rows(normed_one, d_vals),
+        over_rows(d_mid_low, mixed),
+        over_rows(normed_two, d_gate),
+        over_rows(normed_two, d_up),
+        over_rows(cotangent, activated),
+    ]
+    shards = scattered([gains] + [grad.astype(jnp.bfloat16) for grad in grads], "dp")
+    shards = [shard.astype(jnp.float32) for shard in shards]
+    grad_scales = shards[0].reshape(-1)[:gain_size].reshape(1, -1, 2)
+    shards = [shard[None] for shard in shards[1:]]
     (
         grad_query,
         grad_key,
@@ -348,7 +518,6 @@
         grad_gate,
         grad_up,
         grad_down,
-        grad_scales,
     ) = shards
     section_out = lax.dynamic_slice_in_dim(jnp.stack(results), section_index, micros, 0).reshape(
         1, micros, 1, length, width

time: 1280 us -> 823 us (0.64)
  waiting for transfers between devices: 837 us -> 60.7 us
  Pallas kernels: 0 us -> 385 us
  matrix products: 240 us -> 163 us
  local copies, waits for them, and re-layouts: 55.1 us -> 85.5 us
    reduce_scatter x7 -> x0, waiting for transfers between devices: 573 us -> none  [the longest x1 119 us: body(): lax.psum_scatter(ffn_sums[0][None].astype(jnp.bfloat16), 'dp', scatter_di...]
    pallas_call x0 -> x1, Pallas kernels: none -> 385 us  [scattered(): pl.pallas_call(kernel, out_shape=[jax.ShapeDtypeStruct((block, grad.shape...]
    psum x11 -> x0, waiting for transfers between devices: 193 us -> none  [the longest x6 114 us: heads_total(): lax.psum(partial_value.astype(jnp.bfloat16), 'tensor').astype(jnp.float32)]
    dot_general x21 -> x7, matrix products: 96.3 us -> 33.3 us  [over_rows(): lax.dot_general(left, right, (((0,), (0,)), ((), ())), preferred_element_...]
    another operation x2 -> x18, local copies, waits for them, and re-layouts: 0.01 us -> 16.9 us  [the longest x12 10.9 us: body(): jnp.stack(entries)]
    ppermute x4, waiting for transfers between devices: 70.5 us -> 53.6 us  [passed_along(): return lax.ppermute(value, axis, pairs)]
    convert_element_type x8 -> x0, other arithmetic: 14.9 us -> none  [body(): shards = (lax.psum_scatter(attn_sums[0][None].astype(jnp.bfloat16), 'dp',...]
    unnamed x372 -> x395, local copies, waits for them, and re-layouts: 39.3 us -> 32.6 us
  transfers between devices with their start and end apart: 23 -> 16, of which waited for: 22 -> 8; matrix products, arithmetic and copies ran while one was open for 12% -> 15% of each run, Pallas kernels for 0% -> 0%
where the time goes in v1:
time: 823 us; the launch traced here: 810 us
  Pallas kernels  385 us (47%)
  matrix products  163 us (20%)
  other arithmetic  95.8 us (12%)
  local copies, waits for them, and re-layouts  85.5 us (10%)
  waiting for transfers between devices  60.7 us (7%)
  starting transfers between devices  16.9 us (2%)
    pallas_call x1, Pallas kernels, scattered(): pl.pallas_call(kernel, out_shape=[jax.ShapeDtypeStruct((block, grad.shape...  385 us
    ppermute x4, waiting for transfers between devices, passed_along(): return lax.ppermute(value, axis, pairs)  53.6 us
    dot_general x21, matrix products, times_t(): lax.dot_general(left, right, (((1,), (1,)), ((), ())), preferred_element_...  46.2 us
    dot_general x7, matrix products, over_rows(): lax.dot_general(left, right, (((0,), (0,)), ((), ())), preferred_element_...  33.3 us
    unnamed x395, local copies, waits for them, and re-layouts  32.6 us
    another operation x19, other arithmetic, body(): stacked = jax.tree.map(lambda *entries: jnp.stack(entries), *saved)  26.3 us
  transfers between devices with their start and end apart: 16, of which 8 were waited for; matrix products, arithmetic and copies ran while one was open for 15% of the time, Pallas kernels for 0%

profile of v1, /device:TPU:0, one launch (start us, length us, event | category | flops | bytes accessed | tf_op | source)
XLA Modules:
  0.0 810.0 jit_solution(16625895615125391938)
XLA Ops:
  6.6 4.3 copy.131
  30.0 3.4 multiply_convert_fusion.2
  38.2 5.1 collective-permute-start.2
  43.3 16.9 %collective-permute-done.2 = bf16[256,1536]{1,0:T(8,128)(2,1)S(1)} collective-permute-done((bf16[256,1536]{1,0:T(8,128)(2,1)S(1)}, bf16[256,1536]{1,0:T(8,128)(2,1)S(1)}, u32[]{:S(2)}, u32[]{:S(2)}) %collective-permute-start.2) | collective-permute-done | bytes 786464 | tf_op jit(solution)/shard_map/ppermute | solution.py:18
  79.6 3.4 multiply_convert_fusion.1
  91.1 3.8 fusion.415
  94.9 5.6 collective-permute-start.5
  104.8 12.2 %collective-permute-done.5 = bf16[256,1536]{1,0:T(8,128)(2,1)} collective-permute-done((bf16[256,1536]{1,0:T(8,128)(2,1)}, bf16[256,1536]{1,0:T(8,128)(2,1)}, u32[]{:S(2)}, u32[]{:S(2)}) %collective-permute-start.5) | collective-permute-done | bytes 786464 | tf_op jit(solution)/shard_map/ppermute | solution.py:18
  143.4 3.1 fusion.124
  146.5 3.1 fusion.110
  153.4 4.9 fusion.30
  158.4 3.1 multiply_convert_fusion
  171.1 5.4 fusion.16
  176.5 4.8 fusion.56
  206.0 5.7 fusion.65
  218.2 3.4 fusion.181
  221.7 4.6 fusion.411
  228.5 3.1 fusion.96
  231.9 16.8 %collective-permute-done.10 = bf16[256,1536]{1,0:T(8,128)(2,1)S(1)} collective-permute-done((bf16[256,1536]{1,0:T(8,128)(2,1)S(1)}, bf16[256,1536]{1,0:T(8,128)(2,1)S(1)}, u32[]{:S(2)}, u32[]{:S(2)}) %collective-permute-start.10) | collective-permute-done | bytes 786464 | tf_op jit(solution)/shard_map/ppermute | solution.py:18
  248.9 6.6 fusion.116
  303.7 3.1 fusion.169
  316.4 7.7 collective-permute-done.13
  325.6 6.5 fusion.102
  332.0 4.7 fusion.12
  336.8 4.9 fusion.50
  341.9 7.1 bitcast_convert_fusion.2
  349.0 6.7 bitcast_convert_fusion.1
  355.8 6.8 bitcast_convert_fusion
  384.0 5.2 bitcast_convert_fusion.3
  400.2 3.3 bitcast_convert_fusion.4
  407.7 384.5 %shard_map.177 = (bf16[16,128]{1,0:T(8,128)(2,1)}, bf16[192,768]{1,0:T(8,128)(2,1)}, bf16[192,384]{1,0:T(8,128)(2,1)}, bf16[192,384]{1,0:T(8,128)(2,1)}, bf16[19...) custom-call(bf16[2,2,2,16,128]{4,3,2,1,0:T(8,128)(2,1)} %bitcast.921, ...), custom_call_target="tpu_custom_call" | custom-call | tf_op jit(solution)/shard_map/pallas_call | solution.py:222
  806.7 3.1 fusion.166
  (634 shorter events, 243.2 us)
Async XLA Ops:
  0.6 21.6 %copy-start = (bf16[1,1536,768]{2,1,0:T(8,128)(2,1)S(1)}, bf16[1,1536,768]{2,1,0:T(8,128)(2,1)}, u32[]{:S(2)}) copy-start(bf16[1,1536,768]{2,1,0:T(8,128)(2,1)} %param.16) | copy-start | bytes 7077892
  3.6 13.7 %copy-start.143 = (f32[256]{0:T(256)}, f32[256]{0:T(256)S(1)}, u32[]{:S(2)}) copy-start(f32[256]{0:T(256)S(1)} %add_rsqrt_fusion.5) | copy-start | bytes 3076
  23.1 2.5 collective-permute-start
  35.3 2.4 collective-permute-start.1
  38.2 23.7 %copy-start.48 = (bf16[256,1536]{1,0:T(8,128)(2,1)}, bf16[256,1536]{1,0:T(8,128)(2,1)S(1)}, u32[]{:S(2)}) copy-start(bf16[256,1536]{1,0:T(8,128)(2,1)S(1)} %add_convert_fusion.2) | copy-start | bytes 2359300
  38.2 22.4 %copy-start.26 = (bf16[1,1536,384]{2,1,0:T(8,128)(2,1)S(1)}, bf16[1,1536,384]{2,1,0:T(8,128)(2,1)}, u32[]{:S(2)}) copy-start(bf16[1,1536,384]{2,1,0:T(8,128)(2,1)} %param.15) | copy-start | bytes 3538948
  38.2 22.0 %collective-permute-start.2 = (bf16[256,1536]{1,0:T(8,128)(2,1)S(1)}, bf16[256,1536]{1,0:T(8,128)(2,1)S(1)}, u32[]{:S(2)}, u32[]{:S(2)}) collective-permute-start(bf16[256,1536]{1,0:T(8,128)(2,1)S(1)} %add_convert_fusion.2), channel_id=1, source_target_pairs={{0,16},{1,17},{2,18},{3,19},{4,20},{5,21},{6,22},{7,23},{8,24},{9,... | collective-permute-start | bytes 2359304 | tf_op jit(solution)/shard_map/ppermute | solution.py:18
  69.5 7.8 slice-start.20
  72.9 2.4 collective-permute-start.3
  85.8 5.3 collective-permute-start.4
  91.1 9.4 %copy-start.38 = (bf16[2,1,256,1536]{3,2,1,0:T(8,128)(2,1)S(1)}, bf16[2,1,256,1536]{3,2,1,0:T(8,128)(2,1)}, u32[]{:S(2)}) copy-start(bf16[2,1,256,1536]{3,2,1,0:T(8,128)(2,1)} %param.11) | copy-start | bytes 4718596
  94.9 22.2 %collective-permute-start.5 = (bf16[256,1536]{1,0:T(8,128)(2,1)}, bf16[256,1536]{1,0:T(8,128)(2,1)}, u32[]{:S(2)}, u32[]{:S(2)}) collective-permute-start(bf16[256,1536]{1,0:T(8,128)(2,1)} %get-tuple-element.116), channel_id=1, source_target_pairs={{0,16},{1,17},{2,18},{3,19},{4,20},{5,21},{6,22},{7,23},{8,24},{9,... | collective-permute-start | bytes 2359304 | tf_op jit(solution)/shard_map/ppermute | solution.py:18
  104.8 13.8 %copy-start.27 = (bf16[1,1536,384]{2,1,0:T(8,128)(2,1)S(1)}, bf16[1,1536,384]{2,1,0:T(8,128)(2,1)}, u32[]{:S(2)}) copy-start(bf16[1,1536,384]{2,1,0:T(8,128)(2,1)} %param.15) | copy-start | bytes 3538948
  131.4 18.2 %collective-permute-start.6 = (bf16[256,1536]{1,0:T(8,128)(2,1)}, bf16[256,1536]{1,0:T(8,128)(2,1)}, u32[]{:S(2)}, u32[]{:S(2)}) collective-permute-start(bf16[256,1536]{1,0:T(8,128)(2,1)} %convolution_convert_fusion), channel_id=1, source_target_pairs={{0,1},{1,0},{2,3},{3,2},{4,5},{5,4},{6,7},{7,6},{8,9},{9,8},{10,11... | collective-permute-start | bytes 2359304 | tf_op jit(solution)/shard_map/ppermute | solution.py:60
  181.3 2.5 collective-permute-start.8
  205.6 12.6 %collective-permute-start.9 = (bf16[256,1536]{1,0:T(8,128)(2,1)}, bf16[256,1536]{1,0:T(8,128)(2,1)}, u32[]{:S(2)}, u32[]{:S(2)}) collective-permute-start(bf16[256,1536]{1,0:T(8,128)(2,1)} %fusion.47), channel_id=1, source_target_pairs={{0,1},{1,0},{2,3},{3,2},{4,5},{5,4},{6,7},{7,6},{8,9},{9,8},{10,11... | collective-permute-start | bytes 2359304 | tf_op jit(solution)/shard_map/ppermute | solution.py:60
  211.7 10.0 %collective-permute-start.7 = (bf16[256,1536]{1,0:T(8,128)(2,1)}, bf16[256,1536]{1,0:T(8,128)(2,1)}, u32[]{:S(2)}, u32[]{:S(2)}) collective-permute-start(bf16[256,1536]{1,0:T(8,128)(2,1)} %fusion.65), channel_id=1, source_target_pairs={{0,1},{1,0},{2,3},{3,2},{4,5},{5,4},{6,7},{7,6},{8,9},{9,8},{10,11... | collective-permute-start | bytes 2359304 | tf_op jit(solution)/shard_map/ppermute | solution.py:60
  218.1 8.2 %copy-start.5 = (bf16[3,256,1536]{2,1,0:T(8,128)(2,1)}, bf16[3,256,1536]{2,1,0:T(8,128)(2,1)S(1)}, u32[]{:S(2)}) copy-start(bf16[3,256,1536]{2,1,0:T(8,128)(2,1)S(1)} %pad_maximum_fusion.4) | copy-start | bytes 7077892
  226.4 22.3 %collective-permute-start.10 = (bf16[256,1536]{1,0:T(8,128)(2,1)S(1)}, bf16[256,1536]{1,0:T(8,128)(2,1)S(1)}, u32[]{:S(2)}, u32[]{:S(2)}) collective-permute-start(bf16[256,1536]{1,0:T(8,128)(2,1)S(1)} %get-tuple-element.146), channel_id=1, source_target_pairs={{16,0},{17,1},{18,2},{19,3},{20,4},{21,5},{22,6},{23,7},{24,8},{25... | collective-permute-start | bytes 2359304 | tf_op jit(solution)/shard_map/ppermute | solution.py:18
  231.6 17.1 %copy-start.40 = (bf16[2,1,256,1536]{3,2,1,0:T(8,128)(2,1)S(1)}, bf16[2,1,256,1536]{3,2,1,0:T(8,128)(2,1)}, u32[]{:S(2)}) copy-start(bf16[2,1,256,1536]{3,2,1,0:T(8,128)(2,1)} %param.11) | copy-start | bytes 4718596
  231.6 23.9 %slice-start.16 = ((s8[6291456]{0:T(1024)(128)(4,1)}), s8[4194304]{0:T(1024)(128)(4,1)S(1)}, s32[]{:S(2)}) async-start(s8[6291456]{0:T(1024)(128)(4,1)} %bitcast.962), calls=%async_computation.16 | async-start | bytes 8388608
  231.6 25.9 %slice-start.22 = ((s8[6291456]{0:T(1024)(128)(4,1)}), s8[4194304]{0:T(1024)(128)(4,1)S(1)}, s32[]{:S(2)}) async-start(s8[6291456]{0:T(1024)(128)(4,1)} %bitcast.968), calls=%async_computation.22 | async-start | bytes 8388608
  248.8 16.6 %copy-start.46 = (bf16[256,1536]{1,0:T(8,128)(2,1)}, bf16[256,1536]{1,0:T(8,128)(2,1)S(1)}, u32[]{:S(2)}) copy-start(bf16[256,1536]{1,0:T(8,128)(2,1)S(1)} %bitcast_select_fusion.1) | copy-start | bytes 2359300
  248.8 8.7 %slice-start.23 = ((s8[6291456]{0:T(1024)(128)(4,1)}), s8[2097152]{0:T(1024)(128)(4,1)S(1)}, s32[]{:S(2)}) async-start(s8[6291456]{0:T(1024)(128)(4,1)} %bitcast.968), calls=%async_computation.23 | async-start | bytes 4194304
  255.5 8.7 %slice-start = ((s8[4718592]{0:T(1024)(128)(4,1)}), s8[4194304]{0:T(1024)(128)(4,1)S(1)}, s32[]{:S(2)}) async-start(s8[4718592]{0:T(1024)(128)(4,1)} %bitcast.831), calls=%async_computation | async-start | bytes 8388608
  259.4 4.8 collective-permute-start.11
  283.6 12.9 %collective-permute-start.12 = (bf16[256,1536]{1,0:T(8,128)(2,1)}, bf16[256,1536]{1,0:T(8,128)(2,1)}, u32[]{:S(2)}, u32[]{:S(2)}) collective-permute-start(bf16[256,1536]{1,0:T(8,128)(2,1)} %fusion.48), channel_id=1, source_target_pairs={{0,1},{1,0},{2,3},{3,2},{4,5},{5,4},{6,7},{7,6},{8,9},{9,8},{10,11... | collective-permute-start | bytes 2359304 | tf_op jit(solution)/shard_map/ppermute | solution.py:60
  302.4 21.7 %collective-permute-start.13 = (bf16[256,1536]{1,0:T(8,128)(2,1)}, bf16[256,1536]{1,0:T(8,128)(2,1)}, u32[]{:S(2)}, u32[]{:S(2)}) collective-permute-start(bf16[256,1536]{1,0:T(8,128)(2,1)} %fusion.184), channel_id=1, source_target_pairs={{16,0},{17,1},{18,2},{19,3},{20,4},{21,5},{22,6},{23,7},{24,8},{25... | collective-permute-start | bytes 2359304 | tf_op jit(solution)/shard_map/ppermute | solution.py:18
  341.7 20.9 %collective-permute-start.14 = (bf16[256,1536]{1,0:T(8,128)(2,1)S(1)}, bf16[256,1536]{1,0:T(8,128)(2,1)S(1)}, u32[]{:S(2)}, u32[]{:S(2)}) collective-permute-start(bf16[256,1536]{1,0:T(8,128)(2,1)S(1)} %fusion.50), channel_id=1, source_target_pairs={{0,1},{1,0},{2,3},{3,2},{4,5},{5,4},{6,7},{7,6},{8,9},{9,8},{10,11... | collective-permute-start | bytes 2359304 | tf_op jit(solution)/shard_map/ppermute | solution.py:60
  349.0 13.6 %slice-start.2 = ((s8[4718592]{0:T(1024)(128)(4,1)}), s8[4194304]{0:T(1024)(128)(4,1)S(1)}, s32[]{:S(2)}) async-start(s8[4718592]{0:T(1024)(128)(4,1)} %bitcast.833), calls=%async_computation.2 | async-start | bytes 8388608
  381.0 22.5 %collective-permute-start.15 = (bf16[256,1536]{1,0:T(8,128)(2,1)}, bf16[256,1536]{1,0:T(8,128)(2,1)}, u32[]{:S(2)}, u32[]{:S(2)}) collective-permute-start(bf16[256,1536]{1,0:T(8,128)(2,1)} %fusion.49), channel_id=1, source_target_pairs={{0,1},{1,0},{2,3},{3,2},{4,5},{5,4},{6,7},{7,6},{8,9},{9,8},{10,11... | collective-permute-start | bytes 2359304 | tf_op jit(solution)/shard_map/ppermute | solution.py:60
  792.2 7.5 copy-start.110
  (179 other events, 589.3 us)

commit v2 on v1

v2 whole, which is shorter than its diff:
```python
import functools

import jax
import jax.numpy as jnp
import numpy as np
from jax import lax
from jax.experimental import pallas as pl
from jax.experimental.pallas import tpu as pltpu
from jax.sharding import PartitionSpec as P

HEAD_SIZE = 96
HALF = HEAD_SIZE // 2
LANES = 128
HIDDEN_STEPS = 4
SEND_PIECES = 3

EPS = 1e-05
THETA = 100000.0
MESH = pl.DeviceIdType.MESH
MIB = 2**20
SCALE = HEAD_SIZE ** (-0.5)


def rope_tables(length):
    freqs = (THETA ** (-(np.arange(HALF, dtype=np.float64) * 2.0 / HEAD_SIZE))).astype(np.float32)
    angles = np.arange(length, dtype=np.float32)[:, None] * freqs[None, :]
    cosine, sine = np.cos(angles), np.sin(angles)
    room = np.zeros((length, LANES // 2 - HALF), np.float32)
    cosines = np.concatenate([cosine, room, cosine, room], axis=1)
    sines = np.concatenate([-sine, room, sine, room], axis=1)
    return np.stack([cosines, sines]).astype(np.float32)


def dot(left, right):
    return lax.dot_general(
        left, right, (((1,), (0,)), ((), ())), preferred_element_type=jnp.float32
    )


def times_t(left, right):
    return lax.dot_general(
        left, right, (((1,), (1,)), ((), ())), preferred_element_type=jnp.float32
    )


def over_rows(left, right):
    return lax.dot_general(
        left, right, (((0,), (0,)), ((), ())), preferred_element_type=jnp.float32
    )


def spread(values, head):
    room = jnp.zeros((values.shape[0], LANES // 2 - HALF), values.dtype)
    at = head * HEAD_SIZE
    return jnp.concatenate(
        [values[:, at : at + HALF], room, values[:, at + HALF : at + HEAD_SIZE], room], axis=1
    )


def gathered(heads):
    parts = []
    for head in heads:
        parts += [head[:, :HALF], head[:, LANES // 2 : LANES // 2 + HALF]]
    return jnp.concatenate(parts, axis=1)


def turned(values, cosine, sine):
    return values * cosine + pltpu.roll(values, LANES // 2, 1) * sine


def turned_back(values, cosine, sine):
    return values * cosine - pltpu.roll(values, LANES // 2, 1) * sine


def rsqrt_mean(values):
    return lax.rsqrt(jnp.mean(values * values, axis=-1, keepdims=True) + EPS)


class Exchange:
    def __init__(self, number, send, got, send_sem, recv_sem):
        self.number, self.send, self.got = number, send, got
        self.send_sem, self.recv_sem = send_sem, recv_sem
        self.width = send.shape[1] // SEND_PIECES

    def copy(self, piece):
        columns = pl.ds(piece * self.width, self.width)
        return pltpu.make_async_remote_copy(
            src_ref=self.send.at[:, columns],
            dst_ref=self.got.at[self.number, :, columns],
            send_sem=self.send_sem.at[self.number, piece],
            recv_sem=self.recv_sem.at[self.number, piece],
            device_id={"tensor": 1 - lax.axis_index("tensor")},
            device_id_type=MESH,
        )

    def start(self, piece, partial_value):
        columns = pl.ds(piece * self.width, self.width)
        self.send[:, columns] = partial_value.astype(jnp.bfloat16)
        self.copy(piece).start()

    def wait(self):
        for piece in range(SEND_PIECES):
            self.copy(piece).wait()

    def total(self):
        return self.send[...].astype(jnp.float32) + self.got[self.number].astype(jnp.float32)


def half_copy(source, target, rows, send_sem, recv_sem, device):
    return pltpu.make_async_remote_copy(
        src_ref=source.at[rows],
        dst_ref=target.at[rows],
        send_sem=send_sem,
        recv_sem=recv_sem,
        device_id=device,
        device_id_type=MESH,
    )


def passed_on(xin, micro, sems, stage_from):
    tensor = lax.axis_index("tensor")
    rows = xin.shape[1] // 2
    send_sem, recv_sem, pair_send, pair_recv = sems
    slot = xin.at[micro]
    mine = pl.ds(pl.multiple_of(tensor * rows, rows), rows)
    theirs = pl.ds(pl.multiple_of((1 - tensor) * rows, rows), rows)
    half_copy(
        slot, slot, mine, send_sem.at[micro], recv_sem.at[micro], {"pipe": stage_from}
    ).wait_recv()
    copy = half_copy(
        slot, slot, mine, pair_send.at[micro], pair_recv.at[micro], {"tensor": 1 - tensor}
    )
    copy.start()
    half_copy(
        slot, slot, theirs, pair_send.at[micro], pair_recv.at[micro], {"tensor": 1 - tensor}
    ).wait_recv()
    copy.wait_send()


def sent_on(source, xin, micro, sems, stage_to):
    tensor = lax.axis_index("tensor")
    rows = xin.shape[1] // 2
    mine = pl.ds(pl.multiple_of(tensor * rows, rows), rows)
    return half_copy(
        source.at[micro], xin.at[micro], mine, sems[0].at[micro], sems[1].at[micro], {"pipe": stage_to}
    )


def greet(devices):
    barrier = pltpu.get_barrier_semaphore()
    for device in devices:
        pl.semaphore_signal(barrier, inc=1, device_id=device, device_id_type=MESH)
    pl.semaphore_wait(barrier, len(devices))


def forward_kernel(
    own,
    micros,
    inp,
    cot,
    gains,
    tables,
    wq,
    wk,
    wv,
    wo,
    wg,
    wu,
    wd,
    result_out,
    hidden_out,
    n1_out,
    q_out,
    k_out,
    v_out,
    o_out,
    middle_out,
    n2_out,
    gate_out,
    up_out,
    act_out,
    other_out,
    other,
    xin,
    res,
    send,
    got,
    middle,
    acc,
    n2_buf,
    send_sem,
    recv_sem,
    x_send,
    x_recv,
    xp_send,
    xp_recv,
    far_send,
    far_recv,
    near_send,
    near_recv,
):
    micro, step = pl.program_id(0), pl.program_id(1)
    pipe, tensor, data = lax.axis_index("pipe"), lax.axis_index("tensor"), lax.axis_index("dp")
    peers = lax.axis_size("dp")
    partner = lax.rem(data + peers // 2, peers)
    sems = (x_send, x_recv, xp_send, xp_recv)
    length = inp.shape[1]

    def far_copy(source):
        return pltpu.make_async_remote_copy(
            src_ref=source.at[tensor],
            dst_ref=other.at[tensor],
            send_sem=far_send,
            recv_sem=far_recv,
            device_id={"dp": partner},
            device_id_type=MESH,
        )

    def near_copy(which):
        return pltpu.make_async_remote_copy(
            src_ref=other.at[which],
            dst_ref=other.at[which],
            send_sem=near_send,
            recv_sem=near_recv,
            device_id={"tensor": 1 - tensor},
            device_id_type=MESH,
        )

    @pl.when((micro == 0) & (step == 0))
    def _():
        greet([{"tensor": 1 - tensor}, {"pipe": 1 - pipe}, {"dp": partner}])

        @pl.when(pipe == 0)
        def _():
            far_copy(inp).start()

        @pl.when(pipe == 1)
        def _():
            far_copy(cot).start()

    @pl.when((micro == own) & (step == 0))
    def _():
        far_copy(inp).wait()
        near_copy(tensor).start()
        near_copy(1 - tensor).wait_recv()
        near_copy(tensor).wait_send()
        other_out[...] = other[...]

    @pl.when(step == 0)
    def _():
        @pl.when((pipe == 0) & (micro < own))
        def _():
            hidden_out[0] = inp[jnp.minimum(micro, own - 1)]

        @pl.when((pipe == 0) & (micro >= own))
        def _():
            hidden_out[0] = other[jnp.maximum(micro - own, 0)]

        @pl.when(pipe == 1)
        def _():
            passed_on(xin, micro, sems, 0)
            hidden_out[0] = xin[micro]

        wide = hidden_out[0].astype(jnp.float32)
        n1 = (wide * rsqrt_mean(wide) * gains[0:1, :]).astype(jnp.bfloat16)
        n1_out[0] = n1
        query = dot(n1, wq[...])
        keys = dot(n1, wk[...])
        values = dot(n1, wv[...])
        cosine, sine = tables[0], tables[1]
        cosine2 = jnp.concatenate([cosine, cosine], axis=0)
        sine2 = jnp.concatenate([sine, sine], axis=0)
        groups = k_out.shape[1]
        at_q = lax.rem(lax.broadcasted_iota(jnp.int32, (2 * length, length), 0), length)
        at_k = lax.broadcasted_iota(jnp.int32, (2 * length, length), 1)
        causal = at_q >= at_k
        outs = []
        for group in range(groups):
            q = jnp.concatenate([spread(query, 2 * group), spread(query, 2 * group + 1)], axis=0)
            q = turned(q, cosine2, sine2).astype(jnp.bfloat16)
            k = turned(spread(keys, group), cosine, sine).astype(jnp.bfloat16)
            v = spread(values, group).astype(jnp.bfloat16)
            q_out[0, group] = q
            k_out[0, group] = k
            v_out[0, group] = v
            weights = jnp.where(causal, jnp.exp(times_t(q, k) * SCALE), 0.0)
            total = jnp.sum(weights, axis=-1, keepdims=True)
            probs = (weights * (1.0 / total)).astype(jnp.bfloat16)
            mixed = dot(probs, v)
            outs += [mixed[:length], mixed[length:]]
        mixed = gathered(outs).astype(jnp.bfloat16)
        o_out[0] = mixed
        swap = Exchange(2 * micro, send, got, send_sem, recv_sem)
        for piece in range(SEND_PIECES):
            swap.start(piece, times_t(mixed, wo[piece * swap.width : (piece + 1) * swap.width, :]))
        swap.wait()
        both = hidden_out[0].astype(jnp.float32) + swap.total()
        middle[...] = both
        middle_out[0] = both
        n2 = (both * rsqrt_mean(both) * gains[1:2, :]).astype(jnp.bfloat16)
        n2_buf[...] = n2
        n2_out[0] = n2

    @pl.when(step > 0)
    def _():
        n2 = n2_buf[...]
        gate = dot(n2, wg[...])
        up = dot(n2, wu[...])
        act = (gate * jax.nn.sigmoid(gate) * up).astype(jnp.bfloat16)
        gate_out[0] = gate.astype(jnp.bfloat16)
        up_out[0] = up.astype(jnp.bfloat16)
        act_out[0] = act

        @pl.when(step == 1)
        def _():
            acc[...] = times_t(act, wd[...])

        @pl.when((step > 1) & (step < HIDDEN_STEPS))
        def _():
            acc[...] += times_t(act, wd[...])

        @pl.when(step == HIDDEN_STEPS)
        def _():
            swap = Exchange(2 * micro + 1, send, got, send_sem, recv_sem)
            for piece in range(SEND_PIECES):
                columns = slice(piece * swap.width, (piece + 1) * swap.width)
                swap.start(piece, acc[:, columns] + times_t(act, wd[columns, :]))
            swap.wait()
            result = (middle[...] + swap.total()).astype(jnp.bfloat16)
            result_out[0] = result

            @pl.when(pipe == 0)
            def _():
                res[micro] = result
                sent_on(res, xin, micro, sems, 1).start()

            @pl.when((pipe == 0) & (micro == micros - 1))
            def _():
                for which in range(micros):
                    sent_on(res, xin, which, sems, 1).wait_send()


def backward_kernel(
    own,
    micros,
    cot,
    other,
    gains,
    tables,
    hidden,
    q_in,
    k_in,
    v_in,
    middle,
    gate_in,
    up_in,
    wq,
    wk,
    wv,
    wo,
    wg,
    wu,
    wd,
    grad_out,
    g_out,
    low_out,
    dgate_out,
    dup_out,
    dq_out,
    dk_out,
    dv_out,
    gain_out,
    xin,
    res,
    send,
    got,
    d_middle,
    acc,
    send_sem,
    recv_sem,
    x_send,
    x_recv,
    xp_send,
    xp_recv,
):
    micro, step = pl.program_id(0), pl.program_id(1)
    pipe, tensor = lax.axis_index("pipe"), lax.axis_index("tensor")
    sems = (x_send, x_recv, xp_send, xp_recv)
    length = hidden.shape[1]

    @pl.when((micro == 0) & (step == 0))
    def _():
        greet([{"tensor": 1 - tensor}, {"pipe": 1 - pipe}])
        gain_out[...] = jnp.zeros_like(gain_out)

    @pl.when(step == 0)
    def _():
        @pl.when((pipe == 1) & (micro < own))
        def _():
            g_out[0] = cot[jnp.minimum(micro, own - 1)]

        @pl.when((pipe == 1) & (micro >= own))
        def _():
            g_out[0] = other[jnp.maximum(micro - own, 0)]

        @pl.when(pipe == 0)
        def _():
            passed_on(xin, micro, sems, 1)
            g_out[0] = xin[micro]

    @pl.when(step < HIDDEN_STEPS)
    def _():
        d_act = dot(g_out[0], wd[...])
        gate = gate_in[0].astype(jnp.float32)
        up = up_in[0].astype(jnp.float32)
        sig = jax.nn.sigmoid(gate)
        d_gate = (d_act * up * sig * (1.0 + gate * (1.0 - sig))).astype(jnp.bfloat16)
        d_up = (d_act * gate * sig).astype(jnp.bfloat16)
        dgate_out[0] = d_gate
        dup_out[0] = d_up

        @pl.when(step == 0)
        def _():
            acc[...] = times_t(d_gate, wg[...]) + times_t(d_up, wu[...])

        @pl.when((step > 0) & (step < HIDDEN_STEPS - 1))
        def _():
            acc[...] += times_t(d_gate, wg[...]) + times_t(d_up, wu[...])

        @pl.when(step == HIDDEN_STEPS - 1)
        def _():
            swap = Exchange(2 * micro, send, got, send_sem, recv_sem)
            for piece in range(SEND_PIECES):
                columns = slice(piece * swap.width, (piece + 1) * swap.width)
                swap.start(
                    piece,
                    acc[:, columns] + times_t(d_gate, wg[columns, :]) + times_t(d_up, wu[columns, :]),
                )
            swap.wait()
            d_normed = swap.total()
            mid = middle[0]
            scale = rsqrt_mean(mid)
            gain_out[1:2, :] += jnp.sum(d_normed * mid * scale, axis=0, keepdims=True)
            weighted = d_normed * gains[1:2, :]
            inner = jnp.mean(weighted * mid, axis=-1, keepdims=True)
            total = g_out[0].astype(jnp.float32) + scale * weighted - mid * (scale**3 * inner)
            d_middle[...] = total
            low_out[0] = total.astype(jnp.bfloat16)

    @pl.when(step == HIDDEN_STEPS)
    def _():
        d_mixed = dot(low_out[0], wo[...]).astype(jnp.bfloat16).astype(jnp.float32)
        cosine, sine = tables[0], tables[1]
        cosine2 = jnp.concatenate([cosine, cosine], axis=0)
        sine2 = jnp.concatenate([sine, sine], axis=0)
        at_k = lax.broadcasted_iota(jnp.int32, (length, 2 * length), 0)
        at_q = lax.rem(lax.broadcasted_iota(jnp.int32, (length, 2 * length), 1), length)
        causal = at_q >= at_k
        d_queries, d_keys, d_values = [], [], []
        for group in range(k_in.shape[1]):
            q, k, v = q_in[0, group], k_in[0, group], v_in[0, group]
            d_head = jnp.concatenate(
                [spread(d_mixed, 2 * group), spread(d_mixed, 2 * group + 1)], axis=0
            ).astype(jnp.bfloat16)
            weights = jnp.where(causal, jnp.exp(times_t(k, q) * SCALE), 0.0)
            probs = weights * (1.0 / jnp.sum(weights, axis=0, keepdims=True))
            d_probs = times_t(v, d_head)
            moved = probs * d_probs
            delta = jnp.sum(moved, axis=0, keepdims=True)
            d_scores = ((moved - probs * delta) * SCALE).astype(jnp.bfloat16)
            d_values.append(dot(probs.astype(jnp.bfloat16), d_head))
            d_keys.append(turned_back(dot(d_scores, q), cosine, sine))
            d_query = turned_back(over_rows(d_scores, k), cosine2, sine2)
            d_queries += [d_query[:length], d_query[length:]]
        d_query = gathered(d_queries).astype(jnp.bfloat16)
        d_key = gathered(d_keys).astype(jnp.bfloat16)
        d_value = gathered(d_values).astype(jnp.bfloat16)
        dq_out[0] = d_query
        dk_out[0] = d_key
        dv_out[0] = d_value
        swap = Exchange(2 * micro + 1, send, got, send_sem, recv_sem)
        for piece in range(SEND_PIECES):
            rows = slice(piece * swap.width, (piece + 1) * swap.width)
            swap.start(
                piece,
                times_t(d_query, wq[rows, :]) + times_t(d_key, wk[rows, :]) + times_t(d_value, wv[rows, :]),
            )
        swap.wait()
        d_first = swap.total()
        wide = hidden[0].astype(jnp.float32)
        scale = rsqrt_mean(wide)
        gain_out[0:1, :] += jnp.sum(d_first * wide * scale, axis=0, keepdims=True)
        weighted = d_first * gains[0:1, :]
        inner = jnp.mean(weighted * wide, axis=-1, keepdims=True)
        d_hidden = (d_middle[...] + scale * weighted - wide * (scale**3 * inner)).astype(jnp.bfloat16)
        grad_out[0] = d_hidden

        @pl.when(pipe == 1)
        def _():
            res[micro] = d_hidden
            sent_on(res, xin, micro, sems, 0).start()

        @pl.when((pipe == 1) & (micro == micros - 1))
        def _():
            for which in range(micros):
                sent_on(res, xin, which, sems, 0).wait_send()


def forward(inputs, cotangents, gains, tables, weights):
    own, length, width = inputs.shape
    micros = 2 * own
    wq, wk, wv, wo, wg, wu, wd = weights
    groups = wk.shape[1] // HEAD_SIZE
    hidden = wg.shape[1]
    block = hidden // HIDDEN_STEPS
    low, wide = jnp.bfloat16, jnp.float32

    def whole(array):
        return pl.BlockSpec(
            array.shape, lambda m, s: (0,) * array.ndim, pipeline_mode=pl.Buffered(1)
        )

    def streamed(array):
        return pl.BlockSpec((width, block), lambda m, s: (0, jnp.maximum(s - 1, 0)))

    def by_micro(*shape):
        return pl.BlockSpec((1,) + shape, lambda m, s: (m,) + (0,) * len(shape))

    by_block = pl.BlockSpec((1, length, block), lambda m, s: (m, 0, jnp.maximum(s - 1, 0)))
    shapes = [
        ((length, width), low),
        ((length, width), low),
        ((length, width), low),
        ((groups, 2 * length, LANES), low),
        ((groups, length, LANES), low),
        ((groups, length, LANES), low),
        ((length, wq.shape[1]), low),
        ((length, width), wide),
        ((length, width), low),
    ]
    out_shape = [jax.ShapeDtypeStruct((micros,) + shape, kind) for shape, kind in shapes]
    out_specs = [by_micro(*shape) for shape, _ in shapes]
    out_shape += [jax.ShapeDtypeStruct((micros, length, hidden), low)] * 3
    out_specs += [by_block] * 3
    out_shape.append(jax.ShapeDtypeStruct(inputs.shape, low))
    out_specs.append(whole(inputs))
    return pl.pallas_call(
        functools.partial(forward_kernel, own, micros),
        grid=(micros, HIDDEN_STEPS + 1),
        out_shape=out_shape,
        in_specs=[
            whole(inputs),
            pl.BlockSpec(memory_space=pl.ANY),
            whole(gains),
            whole(tables),
            whole(wq),
            whole(wk),
            whole(wv),
            whole(wo),
            streamed(wg),
            streamed(wu),
            streamed(wd),
        ],
        out_specs=out_specs,
        scratch_shapes=[
            pltpu.VMEM((own, length, width), low),
            pltpu.VMEM((micros, length, width), low),
            pltpu.VMEM((micros, length, width), low),
            pltpu.VMEM((length, width), low),
            pltpu.VMEM((2 * micros, length, width), low),
            pltpu.VMEM((length, width), wide),
            pltpu.VMEM((length, width), wide),
            pltpu.VMEM((length, width), low),
            pltpu.SemaphoreType.DMA((2 * micros, SEND_PIECES)),
            pltpu.SemaphoreType.DMA((2 * micros, SEND_PIECES)),
            pltpu.SemaphoreType.DMA((micros,)),
            pltpu.SemaphoreType.DMA((micros,)),
            pltpu.SemaphoreType.DMA((micros,)),
            pltpu.SemaphoreType.DMA((micros,)),
            pltpu.SemaphoreType.DMA,
            pltpu.SemaphoreType.DMA,
            pltpu.SemaphoreType.DMA,
            pltpu.SemaphoreType.DMA,
        ],
        compiler_params=pltpu.CompilerParams(
            collective_id=0, has_side_effects=True, vmem_limit_bytes=62 * MIB
        ),
    )(inputs, cotangents, gains, tables, wq, wk, wv, wo, wg, wu, wd)


def backward(cotangents, other, gains, tables, record, weights):
    own, length, width = cotangents.shape
    micros = 2 * own
    wq, wk, wv, wo, wg, wu, wd = weights
    groups = wk.shape[1] // HEAD_SIZE
    hidden = wg.shape[1]
    block = hidden // HIDDEN_STEPS
    low, wide = jnp.bfloat16, jnp.float32

    def whole(array):
        return pl.BlockSpec(
            array.shape, lambda m, s: (0,) * array.ndim, pipeline_mode=pl.Buffered(1)
        )

    def streamed(array):
        return pl.BlockSpec((width, block), lambda m, s: (0, jnp.minimum(s, HIDDEN_STEPS - 1)))

    def by_micro(*shape):
        return pl.BlockSpec((1,) + shape, lambda m, s: (m,) + (0,) * len(shape))

    by_block = pl.BlockSpec(
        (1, length, block), lambda m, s: (m, 0, jnp.minimum(s, HIDDEN_STEPS - 1))
    )
    shapes = [
        ((length, width), low),
        ((length, width), low),
        ((length, width), low),
        None,
        None,
        ((length, wq.shape[1]), low),
        ((length, wk.shape[1]), low),
        ((length, wv.shape[1]), low),
    ]
    out_shape, out_specs = [], []
    for entry in shapes:
        if entry is None:
            out_shape.append(jax.ShapeDtypeStruct((micros, length, hidden), low))
            out_specs.append(by_block)
        else:
            out_shape.append(jax.ShapeDtypeStruct((micros,) + entry[0], entry[1]))
            out_specs.append(by_micro(*entry[0]))
    out_shape.append(jax.ShapeDtypeStruct(gains.shape, wide))
    out_specs.append(whole(gains))
    return pl.pallas_call(
        functools.partial(backward_kernel, own, micros),
        grid=(micros, HIDDEN_STEPS + 1),
        out_shape=out_shape,
        in_specs=[
            whole(cotangents),
            whole(other),
            whole(gains),
            whole(tables),
            by_micro(length, width),
            by_micro(groups, 2 * length, LANES),
            by_micro(groups, length, LANES),
            by_micro(groups, length, LANES),
            by_micro(length, width),
            by_block,
            by_block,
            whole(wq),
            whole(wk),
            whole(wv),
            whole(wo),
            streamed(wg),
            streamed(wu),
            streamed(wd),
        ],
        out_specs=out_specs,
        scratch_shapes=[
            pltpu.VMEM((micros, length, width), low),
            pltpu.VMEM((micros, length, width), low),
            pltpu.VMEM((length, width), low),
            pltpu.VMEM((2 * micros, length, width), low),
            pltpu.VMEM((length, width), wide),
            pltpu.VMEM((length, width), wide),
            pltpu.SemaphoreType.DMA((2 * micros, SEND_PIECES)),
            pltpu.SemaphoreType.DMA((2 * micros, SEND_PIECES)),
            pltpu.SemaphoreType.DMA((micros,)),
            pltpu.SemaphoreType.DMA((micros,)),
            pltpu.SemaphoreType.DMA((micros,)),
            pltpu.SemaphoreType.DMA((micros,)),
        ],
        compiler_params=pltpu.CompilerParams(
            collective_id=1, has_side_effects=True, vmem_limit_bytes=62 * MIB
        ),
    )(cotangents, other, gains, tables, *record, wq, wk, wv, wo, wg, wu, wd)


WINDOW = 4
LAG = 3


def halving_kernel(widths, blocks, bits, axis, *refs):
    count = len(widths)
    grads, outs = refs[:count], refs[count : 2 * count]
    rest = refs[2 * count :]
    local, got = rest[:count], rest[count : count + count * bits]
    load_sem, send_sem, recv_sem = rest[count + count * bits :]
    me = lax.axis_index(axis)
    own = [lax.rem(lax.div(me, 2**bit), 2) for bit in range(bits)]
    flip = [me + (1 - 2 * own[bit]) * 2**bit for bit in range(bits)]
    greet([{axis: flip[bit]} for bit in range(bits)])
    plain = list(range(bits))
    orders = [plain] if bits < 2 else [plain, [1, 0] + plain[2:]]
    chunks = []
    for which, width in enumerate(widths):
        for at in range(grads[which].shape[-1] // width):
            chunks.append((which, at))
    plans = [orders[number % len(orders)] for number in range(len(chunks))]

    def place(fixed):
        return tuple(fixed[bit] if bit in fixed else slice(None) for bit in reversed(range(bits)))

    loads, sends = {}, {}

    def send(number, level, source, bit):
        which, at = chunks[number]
        copy = pltpu.make_async_remote_copy(
            src_ref=source,
            dst_ref=got[which * bits + level].at[at],
            send_sem=send_sem.at[number, level],
            recv_sem=recv_sem.at[number, level],
            device_id={axis: flip[bit]},
            device_id_type=MESH,
        )
        copy.start()
        sends[number, level] = copy

    def begin(number):
        which, at = chunks[number]
        first = plans[number][0]
        columns = pl.ds(at * widths[which], widths[which])
        send(
            number,
            0,
            grads[which].at[place({first: 1 - own[first]}) + (slice(None), columns)],
            first,
        )
        load = pltpu.make_async_copy(
            grads[which].at[place({first: own[first]}) + (slice(None), columns)],
            local[which].at[at],
            load_sem.at[number],
        )
        load.start()
        loads[number] = load

    def step(number, level):
        which, at = chunks[number]
        order = plans[number]
        width = widths[which]
        block = blocks[which]
        if level == 0:
            loads[number].wait()
        sends[number, level].wait_recv()
        done = order[: level + 1]
        left = [bit for bit in reversed(range(bits)) if bit not in done]
        received = got[which * bits + level].at[at]
        axes = [bit for bit in reversed(range(bits)) if bit != order[0]]
        rows = 64 if block % 64 == 0 else block
        for combo in range(2 ** len(left)):
            fixed = {bit: (combo >> index) & 1 for index, bit in enumerate(left)}
            for bit in done:
                fixed[bit] = own[bit]
            spot = (at,) + tuple(fixed[bit] for bit in axes)
            from_spot = tuple(fixed[bit] for bit in left)

            def add(piece, _):
                where = pl.ds(pl.multiple_of(piece * rows, rows), rows)
                a = local[which][spot + (where, slice(None))].astype(jnp.float32)
                b = received[from_spot + (where, slice(None))].astype(jnp.float32)
                if level == bits - 1:
                    outs[which][where, pl.ds(at * width, width)] = (a + b).astype(jnp.bfloat16)
                else:
                    local[which][spot + (where, slice(None))] = (a + b).astype(jnp.bfloat16)
                return 0

            lax.fori_loop(0, block // rows, add, 0)
        if level < bits - 1:
            following = order[level + 1]
            source = []
            for bit in axes:
                if bit in done:
                    source.append(own[bit])
                elif bit == following:
                    source.append(1 - own[bit])
                else:
                    source.append(slice(None))
            send(number, level + 1, local[which].at[(at,) + tuple(source)], following)

    total = len(chunks)
    for number in range(min(WINDOW, total)):
        begin(number)
    for tick in range(total + LAG * (bits - 1)):
        for level in range(bits):
            number = tick - LAG * level
            if 0 <= number < total:
                step(number, level)
        if tick + WINDOW < total:
            begin(tick + WINDOW)
    for copy in sends.values():
        copy.wait_send()


def scattered(grads, axis, bits):
    blocks = [grad.shape[0] // 2**bits for grad in grads]
    widths = [next(w for w in (256, 384, 128) if grad.shape[1] % w == 0) for grad in grads]
    shaped = [
        grad.reshape((2,) * bits + (block, grad.shape[1])) for grad, block in zip(grads, blocks)
    ]
    pieces = [grad.shape[1] // width for grad, width in zip(grads, widths)]
    scratch = [
        pltpu.VMEM((piece,) + (2,) * (bits - 1) + (block, width), jnp.bfloat16)
        for piece, block, width in zip(pieces, blocks, widths)
    ]
    for piece, block, width in zip(pieces, blocks, widths):
        for level in range(bits):
            scratch.append(
                pltpu.VMEM((piece,) + (2,) * (bits - 1 - level) + (block, width), jnp.bfloat16)
            )
    total = sum(pieces)
    scratch += [
        pltpu.SemaphoreType.DMA((total,)),
        pltpu.SemaphoreType.DMA((total, bits)),
        pltpu.SemaphoreType.DMA((total, bits)),
    ]
    return pl.pallas_call(
        functools.partial(halving_kernel, widths, blocks, bits, axis),
        out_shape=[
            jax.ShapeDtypeStruct((block, grad.shape[1]), jnp.bfloat16)
            for grad, block in zip(grads, blocks)
        ],
        in_specs=[pl.BlockSpec(memory_space=pl.ANY)] * len(grads),
        out_specs=[pl.BlockSpec(memory_space=pltpu.VMEM)] * len(grads),
        scratch_shapes=scratch,
        compiler_params=pltpu.CompilerParams(
            collective_id=2, has_side_effects=True, vmem_limit_bytes=60 * MIB
        ),
    )(*shaped)


def body(
    inputs,
    cotangents,
    norm_scales,
    w_query,
    key_weight,
    value_weight,
    w_out,
    w_gate,
    w_up,
    down_weight,
):
    weights = (
        w_query[0],
        key_weight[0],
        value_weight[0],
        w_out[0],
        w_gate[0],
        w_up[0],
        down_weight[0],
    )
    micros, _, length, width = inputs.shape
    gains = norm_scales[0].T
    tables = jnp.asarray(rope_tables(length))
    cots = cotangents[:, 0]
    (
        result,
        hidden,
        n1,
        q,
        k,
        v,
        mixed,
        middle,
        n2,
        gate,
        up,
        act,
        other,
    ) = forward(inputs[:, 0], cots, gains, tables, weights)
    grad, g, low, d_gate, d_up, d_q, d_k, d_v, gain = backward(
        cots, other, gains, tables, (hidden, q, k, v, middle, gate, up), weights
    )
    peers = lax.axis_size("dp")
    bits = peers.bit_length() - 2
    top = lax.div(lax.axis_index("dp"), peers // 2)

    def rows_of(values):
        flat = values.reshape(-1, values.shape[-1])
        size = flat.shape[-1] // 2
        return lax.dynamic_slice_in_dim(flat, top * size, size, 1)

    def flat(values):
        return values.reshape(-1, values.shape[-1])

    gain_rows = lax.dynamic_slice_in_dim(gain, top * (width // 2), width // 2, 1).T
    gain_rows = gain_rows.astype(jnp.bfloat16).reshape(peers // 2, -1)
    gain_size = gain_rows.shape[1]
    gain_rows = jnp.pad(gain_rows, ((0, 0), (0, 16 * LANES - gain_size))).reshape(-1, LANES)
    n1_rows, n2_rows, low_rows, g_rows = rows_of(n1), rows_of(n2), rows_of(low), rows_of(g)
    grads = [
        over_rows(n2_rows, flat(d_gate)),
        over_rows(n2_rows, flat(d_up)),
        over_rows(g_rows, flat(act)),
        over_rows(n1_rows, flat(d_q)),
        over_rows(n1_rows, flat(d_k)),
        over_rows(n1_rows, flat(d_v)),
        over_rows(low_rows, flat(mixed)),
        gain_rows,
    ]
    shards = scattered([item.astype(jnp.bfloat16) for item in grads], "dp", bits)
    shards = [shard.astype(jnp.float32) for shard in shards]
    grad_scales = shards[7].reshape(-1)[:gain_size].reshape(1, -1, 2)
    grad_gate, grad_up, grad_down, grad_query, grad_key, grad_value, grad_proj = (
        shard[None] for shard in shards[:7]
    )
    return (
        result[:micros][None, :, None],
        grad[:micros][None, :, None],
        grad_scales,
        grad_query,
        grad_key,
        grad_value,
        grad_proj,
        grad_gate,
        grad_up,
        grad_down,
    )


def solution(mesh):
    placed = (
        P(None, "dp", None, None),
        P(None, "dp", None, None),
        P("pipe", None, None),
        P("pipe", None, "tensor"),
        P("pipe", None, "tensor"),
        P("pipe", None, "tensor"),
        P("pipe", None, "tensor"),
        P("pipe", None, "tensor"),
        P("pipe", None, "tensor"),
        P("pipe", None, "tensor"),
    )
    return jax.shard_map(
        body,
        mesh=mesh,
        in_specs=placed,
        out_specs=(
            P("pipe", None, "dp", None, None),
            P("pipe", None, "dp", None, None),
            P("pipe", "dp", None),
            P("pipe", "dp", "tensor"),
            P("pipe", "dp", "tensor"),
            P("pipe", "dp", "tensor"),
            P("pipe", "dp", "tensor"),
            P("pipe", "dp", "tensor"),
            P("pipe", "dp", "tensor"),
            P("pipe", "dp", "tensor"),
        ),
        check_vma=False,
    )
```

time: 823 us -> 393 us (0.48); the launches traced: 810 us -> 393 us
  matrix products: 163 us -> 24.8 us
  other arithmetic: 95.8 us -> 7.41 us
  local copies, waits for them, and re-layouts: 85.5 us -> 7.06 us
  waiting for transfers between devices: 60.7 us -> 0 us
  Pallas kernels: 385 us -> 353 us
  starting transfers between devices: 16.9 us -> 0 us
    dot_general x63 -> x0, matrix products: 130 us -> none  [the longest x21 46.2 us: times_t(): lax.dot_general(left, right, (((1,), (1,)), ((), ())), preferred_element_...]
    ppermute x16 -> x0, waiting for transfers between devices: 60.7 us -> none  [the longest x4 53.6 us: passed_along(): return lax.ppermute(value, axis, pairs)]
    another operation x25 -> x0, other arithmetic: 35.2 us -> none  [the longest x19 26.3 us: body(): stacked = jax.tree.map(lambda *entries: jnp.stack(entries), *saved)]
    pallas_call x1 -> x3, Pallas kernels: 385 us -> 353 us  [the longest x1 145 us: backward(): pl.pallas_call(functools.partial(backward_kernel, own, micros), grid=(mic...]
    unnamed x395 -> x36, local copies, waits for them, and re-layouts: 32.6 us -> 5.78 us
    reduce_sum x17 -> x0, other arithmetic: 21.4 us -> none  [the longest x3 8.27 us: backward_attention(): gain_one = jnp.sum(d_first * wide * scale_one, axis=0)]
    another operation x18 -> x0, local copies, waits for them, and re-layouts: 16.9 us -> none  [the longest x12 10.9 us: body(): jnp.stack(entries)]
    ppermute x16 -> x0, starting transfers between devices: 16.9 us -> none  [the longest x4 13.5 us: passed_along(): return lax.ppermute(value, axis, pairs)]
  transfers between devices with their start and end apart: 16 -> 0, of which waited for: 8 -> 0; matrix products, arithmetic and copies ran while one was open for 15% -> 0% of each run, Pallas kernels for 0% -> 0%
where the time goes in v2:
time: 393 us
  Pallas kernels  353 us (90%)
  matrix products  24.8 us (6%)
  other arithmetic  7.41 us (2%)
  local copies, waits for them, and re-layouts  7.06 us (2%)
    pallas_call x1, Pallas kernels, backward(): pl.pallas_call(functools.partial(backward_kernel, own, micros), grid=(mic...  145 us
    pallas_call x1, Pallas kernels, scattered(): pl.pallas_call(functools.partial(halving_kernel, widths, blocks, bits, ax...  112 us
    pallas_call x1, Pallas kernels, forward(): pl.pallas_call(functools.partial(forward_kernel, own, micros), grid=(micr...  95.1 us
    dot_general x7, matrix products, over_rows(): lax.dot_general(left, right, (((0,), (0,)), ((), ())), preferred_element_...  24.8 us

profile of v2, /device:TPU:0, one launch (start us, length us, event | category | flops | bytes accessed | tf_op | source)
XLA Modules:
  0.0 393.1 jit_solution(16759638272015429350)
XLA Ops:
  0.6 95.1 %shard_map.186 = (bf16[4,256,1536]{2,1,0:T(8,128)(2,1)}, bf16[4,256,1536]{2,1,0:T(8,128)(2,1)}, bf16[4,256,1536]{2,1,0:T(8,128)(2,1)}, bf16[4,4,512,128]{3,2,1,0...) custom-call(bf16[2,256,1536]{2,1,0:T(8,128)(2,1)} %bitcast.91, ...), custom_call_target="tpu_custom_call" | custom-call | tf_op jit(solution)/shard_map/pallas_call | solution.py:547
  95.7 0.0 copy-start.12
  95.8 145.5 %shard_map.187 = (bf16[4,256,1536]{2,1,0:T(8,128)(2,1)}, bf16[4,256,1536]{2,1,0:T(8,128)(2,1)}, bf16[4,256,1536]{2,1,0:T(8,128)(2,1)}, bf16[4,256,2048]{2,1,0:T(...) custom-call(bf16[2,256,1536]{2,1,0:T(8,128)(2,1)} %bitcast.83, ...), custom_call_target="tpu_custom_call" | custom-call | tf_op jit(solution)/shard_map/pallas_call | solution.py:634
  241.3 0.0 copy-done.12
  241.3 0.0 copy-start.10
  241.3 0.0 copy-start.15
  241.3 4.0 %fusion.3 = bf16[768,768]{1,0:T(8,128)(2,1)} fusion(bf16[1024,768]{1,0:T(8,128)(2,1)S(1)} %bitcast.109, bf16[1024,1536]{1,0:T(8,128)(2,1)} %bitcast.108, s32[]{:T(128)S(6)} %select_n.2), kind=kOutput, calls=%fused_computation.8 | convolution fusion | flops 1208549376 | bytes 4325380 | tf_op jit(solution)/shard_map/dot_general | solution.py:47
  245.3 0.0 copy-done.10
  245.3 0.0 copy-done.15
  245.3 1.8 convolution_convert_fusion.4
  247.1 0.0 copy-done.14
  247.1 1.8 convolution_convert_fusion.5
  249.0 0.0 copy-done.13
  249.0 2.5 convolution_convert_fusion.3
  251.5 0.0 copy-done.6
  251.5 1.1 copy-done.11
  252.6 4.9 %convolution_convert_fusion = bf16[768,2048]{1,0:T(8,128)(2,1)} fusion(bf16[1024,2048]{1,0:T(8,128)(2,1)S(1)} %bitcast.99, bf16[1024,1536]{1,0:T(8,128)(2,1)S(1)} %bitcast.107, s32[]{:T(128)S(6)} %select_n.2), kind=kOutput, calls=%fused_computation | convolution fusion | flops 3222798336 | bytes 8912900 | tf_op jit(solution)/shard_map/dot_general | solution.py:47
  257.5 4.9 %convolution_convert_fusion.1 = bf16[768,2048]{1,0:T(8,128)(2,1)} fusion(bf16[1024,2048]{1,0:T(8,128)(2,1)S(1)} %bitcast.101, bf16[1024,1536]{1,0:T(8,128)(2,1)S(1)} %bitcast.102, s32[]{:T(128)S(6)} %select_n.2), kind=kOutput, calls=%fused_computation.1 | convolution fusion | flops 3222798336 | bytes 8912900 | tf_op jit(solution)/shard_map/dot_general | solution.py:47
  262.3 4.9 %convolution_convert_fusion.2 = bf16[768,2048]{1,0:T(8,128)(2,1)} fusion(bf16[1024,2048]{1,0:T(8,128)(2,1)S(1)} %bitcast.100, bf16[1024,1536]{1,0:T(8,128)(2,1)S(1)} %bitcast.103, s32[]{:T(128)S(6)} %select_n.2), kind=kOutput, calls=%fused_computation.2 | convolution fusion | flops 3222798336 | bytes 8912900 | tf_op jit(solution)/shard_map/dot_general | solution.py:47
  267.2 0.7 fusion.11
  267.9 0.2 copy.24
  268.1 0.3 reshape.104
  268.4 0.6 copy.28
  269.0 112.5 %shard_map.188 = (bf16[192,2048]{1,0:T(8,128)(2,1)}, bf16[192,2048]{1,0:T(8,128)(2,1)}, bf16[192,2048]{1,0:T(8,128)(2,1)}, bf16[192,768]{1,0:T(8,128)(2,1)}, bf1...) custom-call(bf16[2,2,192,2048]{3,2,1,0:T(8,128)(2,1)} %bitcast.90, ...), custom_call_target="tpu_custom_call" | custom-call | tf_op jit(solution)/shard_map/pallas_call | solution.py:816
  381.5 3.5 bitcast_convert_fusion
  385.1 0.9 bitcast_convert_fusion.5
  385.9 1.3 bitcast_convert_fusion.2
  387.2 1.1 bitcast_convert_fusion.3
  388.3 0.6 slice_convert_fusion
  388.9 0.1 reshape.108
  389.1 0.7 copy.27
  389.8 3.3 slice_bitcast_fusion
  (23 shorter events, 0.0 us)
Async XLA Ops:
  95.7 145.5 %copy-start.12 = (bf16[4,256,768]{2,1,0:T(8,128)(2,1)S(1)}, bf16[4,256,768]{2,1,0:T(8,128)(2,1)}, u32[]{:S(2)}) copy-start(bf16[4,256,768]{2,1,0:T(8,128)(2,1)} %get-tuple-element.60) | copy-start | bytes 4718596
  241.3 4.0 %copy-start.10 = (bf16[4,256,1536]{2,1,0:T(8,128)(2,1)S(1)}, bf16[4,256,1536]{2,1,0:T(8,128)(2,1)}, u32[]{:S(2)}) copy-start(bf16[4,256,1536]{2,1,0:T(8,128)(2,1)} %get-tuple-element.55) | copy-start | bytes 9437188
  241.3 4.0 %copy-start.15 = (bf16[4,256,384]{2,1,0:T(8,128)(2,1)S(1)}, bf16[4,256,384]{2,1,0:T(8,128)(2,1)}, u32[]{:S(2)}) copy-start(bf16[4,256,384]{2,1,0:T(8,128)(2,1)} %get-tuple-element.58) | copy-start | bytes 2359300
  245.3 1.8 copy-start.14
  247.1 1.8 copy-start.13
  249.0 2.5 copy-start.6
  249.0 3.6 copy-start.11
  252.6 4.9 %copy-start.8 = (bf16[4,256,2048]{2,1,0:T(8,128)(2,1)S(1)}, bf16[4,256,2048]{2,1,0:T(8,128)(2,1)}, u32[]{:S(2)}) copy-start(bf16[4,256,2048]{2,1,0:T(8,128)(2,1)} %get-tuple-element.52) | copy-start | bytes 12582916
  252.6 4.9 %copy-start.9 = (bf16[4,256,1536]{2,1,0:T(8,128)(2,1)S(1)}, bf16[4,256,1536]{2,1,0:T(8,128)(2,1)}, u32[]{:S(2)}) copy-start(bf16[4,256,1536]{2,1,0:T(8,128)(2,1)} %get-tuple-element.50) | copy-start | bytes 9437188
  257.5 4.9 %copy-start.7 = (bf16[4,256,2048]{2,1,0:T(8,128)(2,1)S(1)}, bf16[4,256,2048]{2,1,0:T(8,128)(2,1)}, u32[]{:S(2)}) copy-start(bf16[4,256,2048]{2,1,0:T(8,128)(2,1)} %get-tuple-element.51) | copy-start | bytes 12582916
  381.5 3.6 copy-start.4
  381.5 3.6 copy-start.5
  381.5 4.4 %copy-start.1 = (bf16[192,2048]{1,0:T(8,128)(2,1)S(1)}, bf16[192,2048]{1,0:T(8,128)(2,1)}, u32[]{:S(2)}) copy-start(bf16[192,2048]{1,0:T(8,128)(2,1)} %get-tuple-element.67) | copy-start | bytes 2359300
  381.5 5.7 %copy-start.2 = (bf16[192,768]{1,0:T(8,128)(2,1)S(1)}, bf16[192,768]{1,0:T(8,128)(2,1)}, u32[]{:S(2)}) copy-start(bf16[192,768]{1,0:T(8,128)(2,1)} %get-tuple-element.63) | copy-start | bytes 884740
  381.5 5.7 %copy-start.3 = (bf16[192,768]{1,0:T(8,128)(2,1)S(1)}, bf16[192,768]{1,0:T(8,128)(2,1)}, u32[]{:S(2)}) copy-start(bf16[192,768]{1,0:T(8,128)(2,1)} %get-tuple-element.66) | copy-start | bytes 884740
  385.0 4.7 %copy-start = (bf16[4,256,1536]{2,1,0:T(8,128)(2,1)S(1)}, bf16[4,256,1536]{2,1,0:T(8,128)(2,1)}, u32[]{:S(2)}) copy-start(bf16[4,256,1536]{2,1,0:T(8,128)(2,1)} %get-tuple-element.40) | copy-start | bytes 9437188

commit v3 on v2

--- a/solution.py
+++ b/solution.py
@@ -154,7 +154,6 @@
 
 
 def forward_kernel(
-    own,
     micros,
     inp,
     cot,
@@ -238,7 +237,7 @@
         def _():
             far_copy(cot).start()
 
-    @pl.when((micro == own) & (step == 0))
+    @pl.when((micro == micros - 1) & (step == HIDDEN_STEPS))
     def _():
         far_copy(inp).wait()
         near_copy(tensor).start()
@@ -248,13 +247,9 @@
 
     @pl.when(step == 0)
     def _():
-        @pl.when((pipe == 0) & (micro < own))
-        def _():
-            hidden_out[0] = inp[jnp.minimum(micro, own - 1)]
-
-        @pl.when((pipe == 0) & (micro >= own))
-        def _():
-            hidden_out[0] = other[jnp.maximum(micro - own, 0)]
+        @pl.when(pipe == 0)
+        def _():
+            hidden_out[0] = inp[micro]
 
         @pl.when(pipe == 1)
         def _():
@@ -340,13 +335,38 @@
                     sent_on(res, xin, which, sems, 1).wait_send()
 
 
+def attention_backward(d_mixed, group, q, k, v, trig, causal, with_output):
+    cosine, sine, cosine2, sine2 = trig
+    d_head = jnp.concatenate(
+        [spread(d_mixed, 2 * group), spread(d_mixed, 2 * group + 1)], axis=0
+    ).astype(jnp.bfloat16)
+    weights = jnp.where(causal, jnp.exp(times_t(k, q) * SCALE), 0.0)
+    probs = weights * (1.0 / jnp.sum(weights, axis=0, keepdims=True))
+    moved = probs * times_t(v, d_head)
+    delta = jnp.sum(moved, axis=0, keepdims=True)
+    d_scores = ((moved - probs * delta) * SCALE).astype(jnp.bfloat16)
+    rounded = probs.astype(jnp.bfloat16)
+    d_value = dot(rounded, d_head)
+    d_key = turned_back(dot(d_scores, q), cosine, sine)
+    d_query = turned_back(over_rows(d_scores, k), cosine2, sine2)
+    length = k.shape[0]
+    mixed = over_rows(rounded, v) if with_output else d_query
+    return (
+        [d_query[:length], d_query[length:]],
+        d_key,
+        d_value,
+        [mixed[:length], mixed[length:]],
+    )
+
+
 def backward_kernel(
     own,
-    micros,
     cot,
     other,
     gains,
     tables,
+    n1_own,
+    n2_own,
     hidden,
     q_in,
     k_in,
@@ -369,9 +389,16 @@
     dq_out,
     dk_out,
     dv_out,
+    n1_out,
+    n2_out,
+    act_out,
+    mixed_out,
     gain_out,
     xin,
     res,
+    low_buf,
+    far_buf,
+    far_gain,
     send,
     got,
     d_middle,
@@ -382,42 +409,117 @@
     x_recv,
     xp_send,
     xp_recv,
+    far_send,
+    far_recv,
+    near_send,
+    near_recv,
+    gain_send,
+    gain_recv,
 ):
     micro, step = pl.program_id(0), pl.program_id(1)
-    pipe, tensor = lax.axis_index("pipe"), lax.axis_index("tensor")
+    pipe, tensor, data = lax.axis_index("pipe"), lax.axis_index("tensor"), lax.axis_index("dp")
+    peers = lax.axis_size("dp")
+    partner = lax.rem(data + peers // 2, peers)
     sems = (x_send, x_recv, xp_send, xp_recv)
     length = hidden.shape[1]
+    rows = length // 2
+    mine = pl.ds(pl.multiple_of(tensor * rows, rows), rows)
+    theirs = pl.ds(pl.multiple_of((1 - tensor) * rows, rows), rows)
+    is_own = micro < own
+    late = jnp.maximum(micro - own, 0)
+    early = jnp.minimum(micro, own - 1)
+
+    def far(source, kind, which):
+        return half_copy(
+            source,
+            far_buf.at[kind, which],
+            mine,
+            far_send.at[kind, which],
+            far_recv.at[kind, which],
+            {"dp": partner},
+        )
+
+    def received(kind, which):
+        slot = far_buf.at[kind, which]
+        sem = near_send.at[kind, which], near_recv.at[kind, which], {"tensor": 1 - tensor}
+        far(slot, kind, which).wait_recv()
+        copy = half_copy(slot, slot, mine, *sem)
+        copy.start()
+        half_copy(slot, slot, theirs, *sem).wait_recv()
+        copy.wait_send()
+
+    def gain_copy():
+        return pltpu.make_async_remote_copy(
+            src_ref=gain_out,
+            dst_ref=far_gain,
+            send_sem=gain_send,
+            recv_sem=gain_recv,
+            device_id={"dp": partner},
+            device_id_type=MESH,
+        )
 
     @pl.when((micro == 0) & (step == 0))
     def _():
-        greet([{"tensor": 1 - tensor}, {"pipe": 1 - pipe}])
+        greet([{"tensor": 1 - tensor}, {"pipe": 1 - pipe}, {"dp": partner}])
         gain_out[...] = jnp.zeros_like(gain_out)
-
-    @pl.when(step == 0)
+        for which in range(own):
+            far(n2_own.at[which], 0, which).start()
+
+        @pl.when(pipe == 1)
+        def _():
+            for which in range(own):
+                far(n1_own.at[which], 1, which).start()
+
+    @pl.when(is_own & (step == 0))
     def _():
-        @pl.when((pipe == 1) & (micro < own))
-        def _():
-            g_out[0] = cot[jnp.minimum(micro, own - 1)]
-
-        @pl.when((pipe == 1) & (micro >= own))
-        def _():
-            g_out[0] = other[jnp.maximum(micro - own, 0)]
+        @pl.when(pipe == 1)
+        def _():
+            g_out[0] = cot[early]
 
         @pl.when(pipe == 0)
         def _():
-            passed_on(xin, micro, sems, 1)
-            g_out[0] = xin[micro]
-
-    @pl.when(step < HIDDEN_STEPS)
+            passed_on(xin, early, sems, 1)
+            far(xin.at[early], 1, early).start()
+            g_out[0] = xin[early]
+
+    @pl.when((micro >= own) & (step == 0))
     def _():
+        received(0, late)
+        received(1, late)
+        n2_out[0] = far_buf[0, late]
+
+        @pl.when(pipe == 1)
+        def _():
+            g_out[0] = other[late]
+            n1_out[0] = far_buf[1, late]
+
+        @pl.when(pipe == 0)
+        def _():
+            g_out[0] = far_buf[1, late]
+            wide = other[late].astype(jnp.float32)
+            n1_out[0] = (wide * rsqrt_mean(wide) * gains[0:1, :]).astype(jnp.bfloat16)
+
+    def hidden_grads(gate, up):
         d_act = dot(g_out[0], wd[...])
-        gate = gate_in[0].astype(jnp.float32)
-        up = up_in[0].astype(jnp.float32)
         sig = jax.nn.sigmoid(gate)
         d_gate = (d_act * up * sig * (1.0 + gate * (1.0 - sig))).astype(jnp.bfloat16)
         d_up = (d_act * gate * sig).astype(jnp.bfloat16)
         dgate_out[0] = d_gate
         dup_out[0] = d_up
+        return d_gate, d_up, sig
+
+    @pl.when((micro >= own) & (step < HIDDEN_STEPS))
+    def _():
+        n2 = n2_out[0]
+        gate, up = dot(n2, wg[...]), dot(n2, wu[...])
+        sig = hidden_grads(gate, up)[2]
+        act_out[0] = (gate * sig * up).astype(jnp.bfloat16)
+
+    @pl.when(is_own & (step < HIDDEN_STEPS))
+    def _():
+        d_gate, d_up, _ = hidden_grads(
+            gate_in[0].astype(jnp.float32), up_in[0].astype(jnp.float32)
+        )
 
         @pl.when(step == 0)
         def _():
@@ -445,33 +547,63 @@
             inner = jnp.mean(weighted * mid, axis=-1, keepdims=True)
             total = g_out[0].astype(jnp.float32) + scale * weighted - mid * (scale**3 * inner)
             d_middle[...] = total
-            low_out[0] = total.astype(jnp.bfloat16)
-
-    @pl.when(step == HIDDEN_STEPS)
+            low = total.astype(jnp.bfloat16)
+            low_out[0] = low
+            low_buf[early] = low
+            far(low_buf.at[early], 2, early).start()
+
+    def trig_and_mask():
+        cosine, sine = tables[0], tables[1]
+        trig = (
+            cosine,
+            sine,
+            jnp.concatenate([cosine, cosine], axis=0),
+            jnp.concatenate([sine, sine], axis=0),
+        )
+        at_k = lax.broadcasted_iota(jnp.int32, (length, 2 * length), 0)
+        at_q = lax.rem(lax.broadcasted_iota(jnp.int32, (length, 2 * length), 1), length)
+        return trig, at_q >= at_k
+
+    groups = k_in.shape[1]
+
+    @pl.when((micro >= own) & (step == HIDDEN_STEPS))
+    def _():
+        received(2, late)
+        low = far_buf[2, late]
+        low_out[0] = low
+        n1 = n1_out[0]
+        query, keys, values = dot(n1, wq[...]), dot(n1, wk[...]), dot(n1, wv[...])
+        d_mixed = dot(low, wo[...]).astype(jnp.bfloat16).astype(jnp.float32)
+        trig, causal = trig_and_mask()
+        cosine, sine, cosine2, sine2 = trig
+        d_queries, d_keys, d_values, outs = [], [], [], []
+        for group in range(groups):
+            q = jnp.concatenate([spread(query, 2 * group), spread(query, 2 * group + 1)], axis=0)
+            q = turned(q, cosine2, sine2).astype(jnp.bfloat16)
+            k = turned(spread(keys, group), cosine, sine).astype(jnp.bfloat16)
+            v = spread(values, group).astype(jnp.bfloat16)
+            parts = attention_backward(d_mixed, group, q, k, v, trig, causal, True)
+            d_queries += parts[0]
+            d_keys.append(parts[1])
+            d_values.append(parts[2])
+            outs += parts[3]
+        dq_out[0] = gathered(d_queries).astype(jnp.bfloat16)
+        dk_out[0] = gathered(d_keys).astype(jnp.bfloat16)
+        dv_out[0] = gathered(d_values).astype(jnp.bfloat16)
+        mixed_out[0] = gathered(outs).astype(jnp.bfloat16)
+
+    @pl.when(is_own & (step == HIDDEN_STEPS))
     def _():
         d_mixed = dot(low_out[0], wo[...]).astype(jnp.bfloat16).astype(jnp.float32)
-        cosine, sine = tables[0], tables[1]
-        cosine2 = jnp.concatenate([cosine, cosine], axis=0)
-        sine2 = jnp.concatenate([sine, sine], axis=0)
-        at_k = lax.broadcasted_iota(jnp.int32, (length, 2 * length), 0)
-        at_q = lax.rem(lax.broadcasted_iota(jnp.int32, (length, 2 * length), 1), length)
-        causal = at_q >= at_k
+        trig, causal = trig_and_mask()
         d_queries, d_keys, d_values = [], [], []
-        for group in range(k_in.shape[1]):
-            q, k, v = q_in[0, group], k_in[0, group], v_in[0, group]
-            d_head = jnp.concatenate(
-                [spread(d_mixed, 2 * group), spread(d_mixed, 2 * group + 1)], axis=0
-            ).astype(jnp.bfloat16)
-            weights = jnp.where(causal, jnp.exp(times_t(k, q) * SCALE), 0.0)
-            probs = weights * (1.0 / jnp.sum(weights, axis=0, keepdims=True))
-            d_probs = times_t(v, d_head)
-            moved = probs * d_probs
-            delta = jnp.sum(moved, axis=0, keepdims=True)
-            d_scores = ((moved - probs * delta) * SCALE).astype(jnp.bfloat16)
-            d_values.append(dot(probs.astype(jnp.bfloat16), d_head))
-            d_keys.append(turned_back(dot(d_scores, q), cosine, sine))
-            d_query = turned_back(over_rows(d_scores, k), cosine2, sine2)
-            d_queries += [d_query[:length], d_query[length:]]
+        for group in range(groups):
+            parts = attention_backward(
+                d_mixed, group, q_in[0, group], k_in[0, group], v_in[0, group], trig, causal, False
+            )
+            d_queries += parts[0]
+            d_keys.append(parts[1])
+            d_values.append(parts[2])
         d_query = gathered(d_queries).astype(jnp.bfloat16)
         d_key = gathered(d_keys).astype(jnp.bfloat16)
         d_value = gathered(d_values).astype(jnp.bfloat16)
@@ -480,10 +612,10 @@
         dv_out[0] = d_value
         swap = Exchange(2 * micro + 1, send, got, send_sem, recv_sem)
         for piece in range(SEND_PIECES):
-            rows = slice(piece * swap.width, (piece + 1) * swap.width)
+            part = slice(piece * swap.width, (piece + 1) * swap.width)
             swap.start(
                 piece,
-                times_t(d_query, wq[rows, :]) + times_t(d_key, wk[rows, :]) + times_t(d_value, wv[rows, :]),
+                times_t(d_query, wq[part, :]) + times_t(d_key, wk[part, :]) + times_t(d_value, wv[part, :]),
             )
         swap.wait()
         d_first = swap.total()
@@ -497,18 +629,29 @@
 
         @pl.when(pipe == 1)
         def _():
-            res[micro] = d_hidden
-            sent_on(res, xin, micro, sems, 0).start()
-
-        @pl.when((pipe == 1) & (micro == micros - 1))
-        def _():
-            for which in range(micros):
+            res[early] = d_hidden
+            sent_on(res, xin, early, sems, 0).start()
+
+        @pl.when(micro == own - 1)
+        def _():
+            gain_copy().start()
+
+    @pl.when((micro == 2 * own - 1) & (step == HIDDEN_STEPS))
+    def _():
+        gain_copy().wait()
+        gain_out[...] += far_gain[...]
+        for which in range(own):
+            for kind in range(3):
+                far(low_buf.at[which], kind, which).wait_send()
+
+        @pl.when(pipe == 1)
+        def _():
+            for which in range(own):
                 sent_on(res, xin, which, sems, 0).wait_send()
 
 
 def forward(inputs, cotangents, gains, tables, weights):
-    own, length, width = inputs.shape
-    micros = 2 * own
+    micros, length, width = inputs.shape
     wq, wk, wv, wo, wg, wu, wd = weights
     groups = wk.shape[1] // HEAD_SIZE
     hidden = wg.shape[1]
@@ -545,7 +688,7 @@
     out_shape.append(jax.ShapeDtypeStruct(inputs.shape, low))
     out_specs.append(whole(inputs))
     return pl.pallas_call(
-        functools.partial(forward_kernel, own, micros),
+        functools.partial(forward_kernel, micros),
         grid=(micros, HIDDEN_STEPS + 1),
         out_shape=out_shape,
         in_specs=[
@@ -563,7 +706,7 @@
         ],
         out_specs=out_specs,
         scratch_shapes=[
-            pltpu.VMEM((own, length, width), low),
+            pltpu.VMEM((micros, length, width), low),
             pltpu.VMEM((micros, length, width), low),
             pltpu.VMEM((micros, length, width), low),
             pltpu.VMEM((length, width), low),
@@ -588,13 +731,14 @@
     )(inputs, cotangents, gains, tables, wq, wk, wv, wo, wg, wu, wd)
 
 
-def backward(cotangents, other, gains, tables, record, weights):
+def backward(cotangents, other, gains, tables, n1, n2, record, weights):
     own, length, width = cotangents.shape
     micros = 2 * own
     wq, wk, wv, wo, wg, wu, wd = weights
     groups = wk.shape[1] // HEAD_SIZE
     hidden = wg.shape[1]
     block = hidden // HIDDEN_STEPS
+    last = HIDDEN_STEPS - 1
     low, wide = jnp.bfloat16, jnp.float32
 
     def whole(array):
@@ -603,36 +747,55 @@
         )
 
     def streamed(array):
-        return pl.BlockSpec((width, block), lambda m, s: (0, jnp.minimum(s, HIDDEN_STEPS - 1)))
-
-    def by_micro(*shape):
+        return pl.BlockSpec((width, block), lambda m, s: (0, jnp.minimum(s, last)))
+
+    def of_all(*shape):
         return pl.BlockSpec((1,) + shape, lambda m, s: (m,) + (0,) * len(shape))
 
-    by_block = pl.BlockSpec(
-        (1, length, block), lambda m, s: (m, 0, jnp.minimum(s, HIDDEN_STEPS - 1))
-    )
-    shapes = [
-        ((length, width), low),
-        ((length, width), low),
-        ((length, width), low),
-        None,
-        None,
-        ((length, wq.shape[1]), low),
-        ((length, wk.shape[1]), low),
-        ((length, wv.shape[1]), low),
+    def of_own(*shape):
+        return pl.BlockSpec(
+            (1,) + shape, lambda m, s: (jnp.minimum(m, own - 1),) + (0,) * len(shape)
+        )
+
+    def of_other(*shape):
+        return pl.BlockSpec(
+            (1,) + shape, lambda m, s: (jnp.maximum(m - own, 0),) + (0,) * len(shape)
+        )
+
+    shape = (1, length, block)
+    block_all = pl.BlockSpec(shape, lambda m, s: (m, 0, jnp.minimum(s, last)))
+    block_own = pl.BlockSpec(
+        shape,
+        lambda m, s: (jnp.minimum(m, own - 1), 0, jnp.where(m < own, jnp.minimum(s, last), last)),
+    )
+    block_other = pl.BlockSpec(
+        shape,
+        lambda m, s: (jnp.maximum(m - own, 0), 0, jnp.where(m < own, 0, jnp.minimum(s, last))),
+    )
+    heads, pairs = wq.shape[1], wk.shape[1]
+    outs = [
+        (own, (width,), of_own(length, width)),
+        (micros, (width,), of_all(length, width)),
+        (micros, (width,), of_all(length, width)),
+        (micros, (hidden,), block_all),
+        (micros, (hidden,), block_all),
+        (micros, (heads,), of_all(length, heads)),
+        (micros, (pairs,), of_all(length, pairs)),
+        (micros, (pairs,), of_all(length, pairs)),
+        (own, (width,), of_other(length, width)),
+        (own, (width,), of_other(length, width)),
+        (own, (hidden,), block_other),
+        (own, (heads,), of_other(length, heads)),
     ]
-    out_shape, out_specs = [], []
-    for entry in shapes:
-        if entry is None:
-            out_shape.append(jax.ShapeDtypeStruct((micros, length, hidden), low))
-            out_specs.append(by_block)
-        else:
-            out_shape.append(jax.ShapeDtypeStruct((micros,) + entry[0], entry[1]))
-            out_specs.append(by_micro(*entry[0]))
+    out_shape = [jax.ShapeDtypeStruct((lead, length) + rest, low) for lead, rest, _ in outs]
+    out_specs = [spec for _, _, spec in outs]
     out_shape.append(jax.ShapeDtypeStruct(gains.shape, wide))
     out_specs.append(whole(gains))
+    row = pltpu.SemaphoreType.DMA((own,))
+    grid_of = pltpu.SemaphoreType.DMA((3, own))
+    swaps = pltpu.SemaphoreType.DMA((2 * own, SEND_PIECES))
     return pl.pallas_call(
-        functools.partial(backward_kernel, own, micros),
+        functools.partial(backward_kernel, own),
         grid=(micros, HIDDEN_STEPS + 1),
         out_shape=out_shape,
         in_specs=[
@@ -640,13 +803,15 @@
             whole(other),
             whole(gains),
             whole(tables),
-            by_micro(length, width),
-            by_micro(groups, 2 * length, LANES),
-            by_micro(groups, length, LANES),
-            by_micro(groups, length, LANES),
-            by_micro(length, width),
-            by_block,
-            by_block,
+            pl.BlockSpec(memory_space=pl.ANY),
+            pl.BlockSpec(memory_space=pl.ANY),
+            of_own(length, width),
+            of_own(groups, 2 * length, LANES),
+            of_own(groups, length, LANES),
+            of_own(groups, length, LANES),
+            of_own(length, width),
+            block_own,
+            block_own,
             whole(wq),
             whole(wk),
             whole(wv),
@@ -657,23 +822,32 @@
         ],
         out_specs=out_specs,
         scratch_shapes=[
-            pltpu.VMEM((micros, length, width), low),
-            pltpu.VMEM((micros, length, width), low),
+            pltpu.VMEM((own, length, width), low),
+            pltpu.VMEM((own, length, width), low),
+            pltpu.VMEM((own, length, width), low),
+            pltpu.VMEM((3, own, length, width), low),
+            pltpu.VMEM(gains.shape, wide),
             pltpu.VMEM((length, width), low),
-            pltpu.VMEM((2 * micros, length, width), low),
+            pltpu.VMEM((2 * own, length, width), low),
             pltpu.VMEM((length, width), wide),
             pltpu.VMEM((length, width), wide),
-            pltpu.SemaphoreType.DMA((2 * micros, SEND_PIECES)),
-            pltpu.SemaphoreType.DMA((2 * micros, SEND_PIECES)),
-            pltpu.SemaphoreType.DMA((micros,)),
-            pltpu.SemaphoreType.DMA((micros,)),
-            pltpu.SemaphoreType.DMA((micros,)),
-            pltpu.SemaphoreType.DMA((micros,)),
+            swaps,
+            swaps,
+            row,
+            row,
+            row,
+            row,
+            grid_of,
+            grid_of,
+            grid_of,
+            grid_of,
+            pltpu.SemaphoreType.DMA,
+            pltpu.SemaphoreType.DMA,
         ],
         compiler_params=pltpu.CompilerParams(
             collective_id=1, has_side_effects=True, vmem_limit_bytes=62 * MIB
         ),
-    )(cotangents, other, gains, tables, *record, wq, wk, wv, wo, wg, wu, wd)
+    )(cotangents, other, gains, tables, n1, n2, *record, wq, wk, wv, wo, wg, wu, wd)
 
 
 WINDOW = 4
@@ -868,8 +1042,12 @@
         act,
         other,
     ) = forward(inputs[:, 0], cots, gains, tables, weights)
-    grad, g, low, d_gate, d_up, d_q, d_k, d_v, gain = backward(
-        cots, other, gains, tables, (hidden, q, k, v, middle, gate, up), weights
+    grad, g, low, d_gate, d_up, d_q, d_k, d_v, n1_far, n2_far, act_far, mixed_far, gain = backward(
+        cots, other, gains, tables, n1, n2, (hidden, q, k, v, middle, gate, up), weights
+    )
+    n1, n2, act, mixed = (
+        jnp.concatenate(pair)
+        for pair in ((n1, n1_far), (n2, n2_far), (act, act_far), (mixed, mixed_far))
     )
     peers = lax.axis_size("dp")
     bits = peers.bit_length() - 2
@@ -905,8 +1083,8 @@
         shard[None] for shard in shards[:7]
     )
     return (
-        result[:micros][None, :, None],
-        grad[:micros][None, :, None],
+        result[None, :, None],
+        grad[None, :, None],
         grad_scales,
         grad_query,
         grad_key,

time: 393 us -> 389 us (0.990)
  the two profiles are of different devices: /device:TPU:0 before, /device:TPU:2 now
where the time goes in v3:
time: 389 us; the launch traced here: 381 us
  Pallas kernels  337 us (87%)
  matrix products  24.7 us (6%)
  other arithmetic  11.3 us (3%)
  local copies, waits for them, and re-layouts  6.96 us (2%)
    pallas_call x1, Pallas kernels, backward(): pl.pallas_call(functools.partial(backward_kernel, own), grid=(micros, HID...  141 us
    pallas_call x1, Pallas kernels, scattered(): pl.pallas_call(functools.partial(halving_kernel, widths, blocks, bits, ax...  112 us
    pallas_call x1, Pallas kernels, forward(): pl.pallas_call(functools.partial(forward_kernel, micros), grid=(micros, H...  83.7 us
    dot_general x7, matrix products, over_rows(): lax.dot_general(left, right, (((0,), (0,)), ((), ())), preferred_element_...  24.7 us
    broadcast_in_dim x7, other arithmetic, body(): shard[None]  8.39 us

profile of v3, /device:TPU:2, one launch (start us, length us, event | category | flops | bytes accessed | tf_op | source)
XLA Modules:
  0.0 381.4 jit_solution(10097675897753701717)
XLA Ops:
  0.6 83.7 %shard_map.186 = (bf16[2,256,1536]{2,1,0:T(8,128)(2,1)}, bf16[2,256,1536]{2,1,0:T(8,128)(2,1)}, bf16[2,256,1536]{2,1,0:T(8,128)(2,1)}, bf16[2,4,512,128]{3,2,1,0...) custom-call(bf16[2,256,1536]{2,1,0:T(8,128)(2,1)} %bitcast.95, ...), custom_call_target="tpu_custom_call" | custom-call | tf_op jit(solution)/shard_map/pallas_call | solution.py:690
  84.3 141.4 %shard_map.187 = (bf16[2,256,1536]{2,1,0:T(8,128)(2,1)}, bf16[4,256,1536]{2,1,0:T(8,128)(2,1)}, bf16[4,256,1536]{2,1,0:T(8,128)(2,1)}, bf16[4,256,2048]{2,1,0:T(...) custom-call(bf16[2,256,1536]{2,1,0:T(8,128)(2,1)} %bitcast.81, ...), custom_call_target="tpu_custom_call" | custom-call | tf_op jit(solution)/shard_map/pallas_call | solution.py:797
  225.8 1.3 pad_maximum_fusion.3
  227.1 4.0 %fusion.3 = bf16[768,768]{1,0:T(8,128)(2,1)} fusion(bf16[1024,768]{1,0:T(8,128)(2,1)S(1)} %bitcast.98, bf16[1024,1536]{1,0:T(8,128)(2,1)} %bitcast.109, s32[]{:T(128)S(6)} %select_n.2), kind=kOutput, calls=%fused_computation.10 | convolution fusion | flops 1208549376 | bytes 4325380 | tf_op jit(solution)/shard_map/dot_general | solution.py:47
  231.1 0.0 copy-done.1
  231.1 0.6 pad_maximum_fusion.1
  231.7 0.5 copy-done.20
  232.3 1.8 convolution_convert_fusion.4
  234.1 1.8 convolution_convert_fusion.5
  235.9 2.5 convolution_convert_fusion.3
  238.4 0.4 pad_maximum_fusion
  238.8 1.5 copy-done.17
  240.3 4.8 %convolution_convert_fusion = bf16[768,2048]{1,0:T(8,128)(2,1)} fusion(bf16[1024,2048]{1,0:T(8,128)(2,1)S(1)} %bitcast.86, bf16[1024,1536]{1,0:T(8,128)(2,1)S(1)} %bitcast.108, s32[]{:T(128)S(6)} %select_n.2), kind=kOutput, calls=%fused_computation.1 | convolution fusion | flops 3222798336 | bytes 8912900 | tf_op jit(solution)/shard_map/dot_general | solution.py:47
  245.1 4.9 %convolution_convert_fusion.1 = bf16[768,2048]{1,0:T(8,128)(2,1)} fusion(bf16[1024,2048]{1,0:T(8,128)(2,1)S(1)} %bitcast.107, bf16[1024,1536]{1,0:T(8,128)(2,1)S(1)} %bitcast.90, s32[]{:T(128)S(6)} %select_n.2), kind=kOutput, calls=%fused_computation.2 | convolution fusion | flops 3222798336 | bytes 8912900 | tf_op jit(solution)/shard_map/dot_general | solution.py:47
  250.0 4.8 %convolution_convert_fusion.2 = bf16[768,2048]{1,0:T(8,128)(2,1)} fusion(bf16[1024,2048]{1,0:T(8,128)(2,1)S(1)} %bitcast.106, bf16[1024,1536]{1,0:T(8,128)(2,1)S(1)} %bitcast.91, s32[]{:T(128)S(6)} %select_n.2), kind=kOutput, calls=%fused_computation.3 | convolution fusion | flops 3222798336 | bytes 8912900 | tf_op jit(solution)/shard_map/dot_general | solution.py:47
  254.8 0.7 fusion.11
  255.5 0.2 copy.24
  255.7 0.3 reshape.104
  256.0 0.6 copy.28
  256.6 112.4 %shard_map.188 = (bf16[192,2048]{1,0:T(8,128)(2,1)}, bf16[192,2048]{1,0:T(8,128)(2,1)}, bf16[192,2048]{1,0:T(8,128)(2,1)}, bf16[192,768]{1,0:T(8,128)(2,1)}, bf1...) custom-call(bf16[2,2,192,2048]{3,2,1,0:T(8,128)(2,1)} %bitcast.89, ...), custom_call_target="tpu_custom_call" | custom-call | tf_op jit(solution)/shard_map/pallas_call | solution.py:990
  369.0 2.6 bitcast_convert_fusion
  371.6 1.3 bitcast_convert_fusion.1
  372.9 1.3 bitcast_convert_fusion.2
  374.3 0.9 bitcast_convert_fusion.3
  375.1 0.9 bitcast_convert_fusion.4
  376.0 0.7 bitcast_convert_fusion.5
  376.7 0.7 bitcast_convert_fusion.6
  377.5 0.7 slice_convert_fusion
  378.1 0.1 reshape.108
  378.3 0.7 copy.27
  378.9 1.1 copy.31
  380.1 1.1 copy.32
  (40 shorter events, 0.1 us)
Async XLA Ops:
  84.3 141.4 %copy-start.8 = (bf16[2,256,768]{2,1,0:T(8,128)(2,1)S(1)}, bf16[2,256,768]{2,1,0:T(8,128)(2,1)}, u32[]{:S(2)}) copy-start(bf16[2,256,768]{2,1,0:T(8,128)(2,1)} %get-tuple-element.67) | copy-start | bytes 2359300
  227.0 4.1 %copy-start = (bf16[2,256,1536]{2,1,0:T(8,128)(2,1)S(1)}, bf16[2,256,1536]{2,1,0:T(8,128)(2,1)}, u32[]{:S(2)}) copy-start(bf16[2,256,1536]{2,1,0:T(8,128)(2,1)} %get-tuple-element.46.n1_own) | copy-start | bytes 4718596
  227.1 4.1 %copy-start.1 = (bf16[2,256,1536]{2,1,0:T(8,128)(2,1)S(1)}, bf16[2,256,1536]{2,1,0:T(8,128)(2,1)}, u32[]{:S(2)}) copy-start(bf16[2,256,1536]{2,1,0:T(8,128)(2,1)} %get-tuple-element.47.n2_own) | copy-start | bytes 4718596
  227.1 4.0 %copy-start.4 = (bf16[2,256,1536]{2,1,0:T(8,128)(2,1)S(1)}, bf16[2,256,1536]{2,1,0:T(8,128)(2,1)}, u32[]{:S(2)}) copy-start(bf16[2,256,1536]{2,1,0:T(8,128)(2,1)} %get-tuple-element.62) | copy-start | bytes 4718596
  227.1 4.0 %copy-start.5 = (bf16[2,256,1536]{2,1,0:T(8,128)(2,1)S(1)}, bf16[2,256,1536]{2,1,0:T(8,128)(2,1)}, u32[]{:S(2)}) copy-start(bf16[2,256,1536]{2,1,0:T(8,128)(2,1)} %get-tuple-element.56) | copy-start | bytes 4718596
  231.1 1.1 copy-start.20
  232.3 1.8 copy-start.19
  234.1 1.8 copy-start.18
  235.9 2.5 copy-start.2
  235.9 2.5 copy-start.3
  238.4 1.9 copy-start.17
  240.3 4.9 %copy-start.16 = (bf16[4,256,2048]{2,1,0:T(8,128)(2,1)S(1)}, bf16[4,256,2048]{2,1,0:T(8,128)(2,1)}, u32[]{:S(2)}) copy-start(bf16[4,256,2048]{2,1,0:T(8,128)(2,1)} %get-tuple-element.58) | copy-start | bytes 12582916
  245.1 4.9 %copy-start.15 = (bf16[4,256,2048]{2,1,0:T(8,128)(2,1)S(1)}, bf16[4,256,2048]{2,1,0:T(8,128)(2,1)}, u32[]{:S(2)}) copy-start(bf16[4,256,2048]{2,1,0:T(8,128)(2,1)} %get-tuple-element.57) | copy-start | bytes 12582916
  369.0 2.6 copy-start.10
  369.0 3.9 %copy-start.9 = (bf16[192,2048]{1,0:T(8,128)(2,1)S(1)}, bf16[192,2048]{1,0:T(8,128)(2,1)}, u32[]{:S(2)}) copy-start(bf16[192,2048]{1,0:T(8,128)(2,1)} %get-tuple-element.75) | copy-start | bytes 2359300
  371.6 2.7 copy-start.12
  372.9 2.2 copy-start.11
  372.9 3.1 copy-start.14
  372.9 3.8 copy-start.13
  372.9 6.0 %copy-start.6 = (bf16[2,256,1536]{2,1,0:T(8,128)(2,1)S(1)}, bf16[2,256,1536]{2,1,0:T(8,128)(2,1)}, u32[]{:S(2)}) copy-start(bf16[2,256,1536]{2,1,0:T(8,128)(2,1)} %get-tuple-element.44) | copy-start | bytes 4718596
  376.0 4.1 %copy-start.7 = (bf16[2,256,1536]{2,1,0:T(8,128)(2,1)S(1)}, bf16[2,256,1536]{2,1,0:T(8,128)(2,1)}, u32[]{:S(2)}) copy-start(bf16[2,256,1536]{2,1,0:T(8,128)(2,1)} %get-tuple-element.55) | copy-start | bytes 4718596

commit v4 on v2

--- a/solution.py
+++ b/solution.py
@@ -153,8 +153,36 @@
     pl.semaphore_wait(barrier, len(devices))
 
 
+class FarCopies:
+    def __init__(self, sources, buffers, sems, partner):
+        self.sources, self.buffers, self.sems, self.partner = sources, buffers, sems, partner
+        tensor = lax.axis_index("tensor")
+        self.pair = {"tensor": 1 - tensor}
+        rows = buffers.shape[1] // 2
+        self.mine = pl.ds(pl.multiple_of(tensor * rows, rows), rows)
+        self.theirs = pl.ds(pl.multiple_of((1 - tensor) * rows, rows), rows)
+
+    def far(self, which, source=None):
+        source = self.sources.at[which] if source is None else source
+        sems = self.sems.at[which, 0], self.sems.at[which, 1]
+        return half_copy(source, self.buffers.at[which], self.mine, *sems, {"dp": self.partner})
+
+    def near(self, which, rows):
+        slot = self.buffers.at[which]
+        sems = self.sems.at[which, 2], self.sems.at[which, 3]
+        return half_copy(slot, slot, rows, *sems, self.pair)
+
+    def start(self, which, source=None):
+        self.far(which, source).start()
+
+    def receive(self, which):
+        self.far(which, self.buffers.at[which]).wait()
+        self.near(which, self.mine).start()
+        self.near(which, self.theirs).wait_recv()
+        self.near(which, self.mine).wait_send()
+
+
 def forward_kernel(
-    own,
     micros,
     inp,
     cot,
@@ -180,7 +208,10 @@
     up_out,
     act_out,
     other_out,
+    far_out,
     other,
+    first_buf,
+    far_buf,
     xin,
     res,
     send,
@@ -198,6 +229,7 @@
     far_recv,
     near_send,
     near_recv,
+    far_sems,
 ):
     micro, step = pl.program_id(0), pl.program_id(1)
     pipe, tensor, data = lax.axis_index("pipe"), lax.axis_index("tensor"), lax.axis_index("dp")
@@ -226,6 +258,8 @@
             device_id_type=MESH,
         )
 
+    far = FarCopies(first_buf, far_buf, far_sems, partner)
+
     @pl.when((micro == 0) & (step == 0))
     def _():
         greet([{"tensor": 1 - tensor}, {"pipe": 1 - pipe}, {"dp": partner}])
@@ -238,23 +272,30 @@
         def _():
             far_copy(cot).start()
 
-    @pl.when((micro == own) & (step == 0))
+    @pl.when((micro == micros - 1) & (step == HIDDEN_STEPS))
     def _():
         far_copy(inp).wait()
         near_copy(tensor).start()
         near_copy(1 - tensor).wait_recv()
         near_copy(tensor).wait_send()
         other_out[...] = other[...]
+        far.receive(1)
+        far_out[1] = far_buf[1]
+
+        @pl.when(pipe == 1)
+        def _():
+            far.receive(0)
+            far_out[0] = far_buf[0]
+
+        @pl.when(pipe == 0)
+        def _():
+            far_out[0] = jnp.zeros_like(far_out[0])
 
     @pl.when(step == 0)
     def _():
-        @pl.when((pipe == 0) & (micro < own))
-        def _():
-            hidden_out[0] = inp[jnp.minimum(micro, own - 1)]
-
-        @pl.when((pipe == 0) & (micro >= own))
-        def _():
-            hidden_out[0] = other[jnp.maximum(micro - own, 0)]
+        @pl.when(pipe == 0)
+        def _():
+            hidden_out[0] = inp[micro]
 
         @pl.when(pipe == 1)
         def _():
@@ -264,6 +305,12 @@
         wide = hidden_out[0].astype(jnp.float32)
         n1 = (wide * rsqrt_mean(wide) * gains[0:1, :]).astype(jnp.bfloat16)
         n1_out[0] = n1
+
+        @pl.when((pipe == 1) & (micro == 0))
+        def _():
+            first_buf[0] = n1
+            far.start(0)
+
         query = dot(n1, wq[...])
         keys = dot(n1, wk[...])
         values = dot(n1, wv[...])
@@ -301,6 +348,12 @@
         n2_buf[...] = n2
         n2_out[0] = n2
 
+        @pl.when(micro == 0)
+        def _():
+            first_buf[1] = n2
+            far.start(1)
+
+
     @pl.when(step > 0)
     def _():
         n2 = n2_buf[...]
@@ -340,13 +393,39 @@
                     sent_on(res, xin, which, sems, 1).wait_send()
 
 
+def attention_backward(d_mixed, group, q, k, v, trig, causal, with_output):
+    cosine, sine, cosine2, sine2 = trig
+    d_head = jnp.concatenate(
+        [spread(d_mixed, 2 * group), spread(d_mixed, 2 * group + 1)], axis=0
+    ).astype(jnp.bfloat16)
+    weights = jnp.where(causal, jnp.exp(times_t(k, q) * SCALE), 0.0)
+    probs = weights * (1.0 / jnp.sum(weights, axis=0, keepdims=True))
+    moved = probs * times_t(v, d_head)
+    delta = jnp.sum(moved, axis=0, keepdims=True)
+    d_scores = ((moved - probs * delta) * SCALE).astype(jnp.bfloat16)
+    rounded = probs.astype(jnp.bfloat16)
+    d_value = dot(rounded, d_head)
+    d_key = turned_back(dot(d_scores, q), cosine, sine)
+    d_query = turned_back(over_rows(d_scores, k), cosine2, sine2)
+    length = k.shape[0]
+    mixed = over_rows(rounded, v) if with_output else d_query
+    return (
+        [d_query[:length], d_query[length:]],
+        d_key,
+        d_value,
+        [mixed[:length], mixed[length:]],
+    )
+
+
 def backward_kernel(
-    own,
     micros,
     cot,
     other,
+    far_first,
     gains,
     tables,
+    n1_own,
+    n2_own,
     hidden,
     q_in,
     k_in,
@@ -369,9 +448,14 @@
     dq_out,
     dk_out,
     dv_out,
+    n1_far,
+    n2_far,
+    g_far,
     gain_out,
     xin,
     res,
+    far_buf,
+    far_gain,
     send,
     got,
     d_middle,
@@ -382,37 +466,67 @@
     x_recv,
     xp_send,
     xp_recv,
+    far_sems,
+    gain_send,
+    gain_recv,
 ):
     micro, step = pl.program_id(0), pl.program_id(1)
-    pipe, tensor = lax.axis_index("pipe"), lax.axis_index("tensor")
+    pipe, tensor, data = lax.axis_index("pipe"), lax.axis_index("tensor"), lax.axis_index("dp")
+    peers = lax.axis_size("dp")
+    partner = lax.rem(data + peers // 2, peers)
     sems = (x_send, x_recv, xp_send, xp_recv)
     length = hidden.shape[1]
+    last = micros - 1
+    far = FarCopies(xin, far_buf, far_sems, partner)
+
+    def gain_copy():
+        return pltpu.make_async_remote_copy(
+            src_ref=gain_out,
+            dst_ref=far_gain,
+            send_sem=gain_send,
+            recv_sem=gain_recv,
+            device_id={"dp": partner},
+            device_id_type=MESH,
+        )
 
     @pl.when((micro == 0) & (step == 0))
     def _():
-        greet([{"tensor": 1 - tensor}, {"pipe": 1 - pipe}])
+        greet([{"tensor": 1 - tensor}, {"pipe": 1 - pipe}, {"dp": partner}])
         gain_out[...] = jnp.zeros_like(gain_out)
+        for which in range(1, micros):
+            far.start(micros + which, n2_own.at[which])
+
+        @pl.when(pipe == 1)
+        def _():
+            for which in range(1, micros):
+                far.start(which, n1_own.at[which])
+            g_far[...] = other[...]
+            n1_far[0] = far_first[0]
+
+        @pl.when(pipe == 0)
+        def _():
+            for which in range(micros):
+                wide = other[which].astype(jnp.float32)
+                n1_far[which] = (wide * rsqrt_mean(wide) * gains[0:1, :]).astype(jnp.bfloat16)
+
+        n2_far[0] = far_first[1]
 
     @pl.when(step == 0)
     def _():
-        @pl.when((pipe == 1) & (micro < own))
-        def _():
-            g_out[0] = cot[jnp.minimum(micro, own - 1)]
-
-        @pl.when((pipe == 1) & (micro >= own))
-        def _():
-            g_out[0] = other[jnp.maximum(micro - own, 0)]
+        @pl.when(pipe == 1)
+        def _():
+            g_out[0] = cot[micro]
 
         @pl.when(pipe == 0)
         def _():
             passed_on(xin, micro, sems, 1)
+            far.start(micro)
             g_out[0] = xin[micro]
 
     @pl.when(step < HIDDEN_STEPS)
     def _():
+        gate, up = gate_in[0].astype(jnp.float32), up_in[0].astype(jnp.float32)
         d_act = dot(g_out[0], wd[...])
-        gate = gate_in[0].astype(jnp.float32)
-        up = up_in[0].astype(jnp.float32)
         sig = jax.nn.sigmoid(gate)
         d_gate = (d_act * up * sig * (1.0 + gate * (1.0 - sig))).astype(jnp.bfloat16)
         d_up = (d_act * gate * sig).astype(jnp.bfloat16)
@@ -450,28 +564,15 @@
     @pl.when(step == HIDDEN_STEPS)
     def _():
         d_mixed = dot(low_out[0], wo[...]).astype(jnp.bfloat16).astype(jnp.float32)
-        cosine, sine = tables[0], tables[1]
-        cosine2 = jnp.concatenate([cosine, cosine], axis=0)
-        sine2 = jnp.concatenate([sine, sine], axis=0)
-        at_k = lax.broadcasted_iota(jnp.int32, (length, 2 * length), 0)
-        at_q = lax.rem(lax.broadcasted_iota(jnp.int32, (length, 2 * length), 1), length)
-        causal = at_q >= at_k
+        trig, causal = trig_and_mask(tables, length)
         d_queries, d_keys, d_values = [], [], []
         for group in range(k_in.shape[1]):
-            q, k, v = q_in[0, group], k_in[0, group], v_in[0, group]
-            d_head = jnp.concatenate(
-                [spread(d_mixed, 2 * group), spread(d_mixed, 2 * group + 1)], axis=0
-            ).astype(jnp.bfloat16)
-            weights = jnp.where(causal, jnp.exp(times_t(k, q) * SCALE), 0.0)
-            probs = weights * (1.0 / jnp.sum(weights, axis=0, keepdims=True))
-            d_probs = times_t(v, d_head)
-            moved = probs * d_probs
-            delta = jnp.sum(moved, axis=0, keepdims=True)
-            d_scores = ((moved - probs * delta) * SCALE).astype(jnp.bfloat16)
-            d_values.append(dot(probs.astype(jnp.bfloat16), d_head))
-            d_keys.append(turned_back(dot(d_scores, q), cosine, sine))
-            d_query = turned_back(over_rows(d_scores, k), cosine2, sine2)
-            d_queries += [d_query[:length], d_query[length:]]
+            parts = attention_backward(
+                d_mixed, group, q_in[0, group], k_in[0, group], v_in[0, group], trig, causal, False
+            )
+            d_queries += parts[0]
+            d_keys.append(parts[1])
+            d_values.append(parts[2])
         d_query = gathered(d_queries).astype(jnp.bfloat16)
         d_key = gathered(d_keys).astype(jnp.bfloat16)
         d_value = gathered(d_values).astype(jnp.bfloat16)
@@ -480,10 +581,10 @@
         dv_out[0] = d_value
         swap = Exchange(2 * micro + 1, send, got, send_sem, recv_sem)
         for piece in range(SEND_PIECES):
-            rows = slice(piece * swap.width, (piece + 1) * swap.width)
+            part = slice(piece * swap.width, (piece + 1) * swap.width)
             swap.start(
                 piece,
-                times_t(d_query, wq[rows, :]) + times_t(d_key, wk[rows, :]) + times_t(d_value, wv[rows, :]),
+                times_t(d_query, wq[part, :]) + times_t(d_key, wk[part, :]) + times_t(d_value, wv[part, :]),
             )
         swap.wait()
         d_first = swap.total()
@@ -500,15 +601,49 @@
             res[micro] = d_hidden
             sent_on(res, xin, micro, sems, 0).start()
 
-        @pl.when((pipe == 1) & (micro == micros - 1))
-        def _():
-            for which in range(micros):
-                sent_on(res, xin, which, sems, 0).wait_send()
+        @pl.when(micro == last)
+        def _():
+            gain_copy().start()
+            for which in range(1, micros):
+                far.receive(micros + which)
+                n2_far[which] = far_buf[micros + which]
+
+            @pl.when(pipe == 1)
+            def _():
+                for which in range(1, micros):
+                    far.receive(which)
+                    n1_far[which] = far_buf[which]
+
+            @pl.when(pipe == 0)
+            def _():
+                for which in range(micros):
+                    far.receive(which)
+                    g_far[which] = far_buf[which]
+
+            gain_copy().wait()
+            gain_out[...] += far_gain[...]
+
+            @pl.when(pipe == 1)
+            def _():
+                for which in range(micros):
+                    sent_on(res, xin, which, sems, 0).wait_send()
+
+
+def trig_and_mask(tables, length):
+    cosine, sine = tables[0], tables[1]
+    trig = (
+        cosine,
+        sine,
+        jnp.concatenate([cosine, cosine], axis=0),
+        jnp.concatenate([sine, sine], axis=0),
+    )
+    at_k = lax.broadcasted_iota(jnp.int32, (length, 2 * length), 0)
+    at_q = lax.rem(lax.broadcasted_iota(jnp.int32, (length, 2 * length), 1), length)
+    return trig, at_q >= at_k
 
 
 def forward(inputs, cotangents, gains, tables, weights):
-    own, length, width = inputs.shape
-    micros = 2 * own
+    micros, length, width = inputs.shape
     wq, wk, wv, wo, wg, wu, wd = weights
     groups = wk.shape[1] // HEAD_SIZE
     hidden = wg.shape[1]
@@ -542,10 +677,10 @@
     out_specs = [by_micro(*shape) for shape, _ in shapes]
     out_shape += [jax.ShapeDtypeStruct((micros, length, hidden), low)] * 3
     out_specs += [by_block] * 3
-    out_shape.append(jax.ShapeDtypeStruct(inputs.shape, low))
-    out_specs.append(whole(inputs))
+    out_shape += [jax.ShapeDtypeStruct(inputs.shape, low)] * 2
+    out_specs += [whole(inputs)] * 2
     return pl.pallas_call(
-        functools.partial(forward_kernel, own, micros),
+        functools.partial(forward_kernel, micros),
         grid=(micros, HIDDEN_STEPS + 1),
         out_shape=out_shape,
         in_specs=[
@@ -563,7 +698,9 @@
         ],
         out_specs=out_specs,
         scratch_shapes=[
-            pltpu.VMEM((own, length, width), low),
+            pltpu.VMEM((micros, length, width), low),
+            pltpu.VMEM((2, length, width), low),
+            pltpu.VMEM((2, length, width), low),
             pltpu.VMEM((micros, length, width), low),
             pltpu.VMEM((micros, length, width), low),
             pltpu.VMEM((length, width), low),
@@ -581,6 +718,7 @@
             pltpu.SemaphoreType.DMA,
             pltpu.SemaphoreType.DMA,
             pltpu.SemaphoreType.DMA,
+            pltpu.SemaphoreType.DMA((2, 4)),
         ],
         compiler_params=pltpu.CompilerParams(
             collective_id=0, has_side_effects=True, vmem_limit_bytes=62 * MIB
@@ -588,13 +726,13 @@
     )(inputs, cotangents, gains, tables, wq, wk, wv, wo, wg, wu, wd)
 
 
-def backward(cotangents, other, gains, tables, record, weights):
-    own, length, width = cotangents.shape
-    micros = 2 * own
+def backward(cotangents, other, far_first, gains, tables, n1, n2, record, weights):
+    micros, length, width = cotangents.shape
     wq, wk, wv, wo, wg, wu, wd = weights
     groups = wk.shape[1] // HEAD_SIZE
     hidden = wg.shape[1]
     block = hidden // HIDDEN_STEPS
+    last = HIDDEN_STEPS - 1
     low, wide = jnp.bfloat16, jnp.float32
 
     def whole(array):
@@ -603,43 +741,32 @@
         )
 
     def streamed(array):
-        return pl.BlockSpec((width, block), lambda m, s: (0, jnp.minimum(s, HIDDEN_STEPS - 1)))
+        return pl.BlockSpec((width, block), lambda m, s: (0, jnp.minimum(s, last)))
 
     def by_micro(*shape):
         return pl.BlockSpec((1,) + shape, lambda m, s: (m,) + (0,) * len(shape))
 
-    by_block = pl.BlockSpec(
-        (1, length, block), lambda m, s: (m, 0, jnp.minimum(s, HIDDEN_STEPS - 1))
-    )
-    shapes = [
-        ((length, width), low),
-        ((length, width), low),
-        ((length, width), low),
-        None,
-        None,
-        ((length, wq.shape[1]), low),
-        ((length, wk.shape[1]), low),
-        ((length, wv.shape[1]), low),
-    ]
-    out_shape, out_specs = [], []
-    for entry in shapes:
-        if entry is None:
-            out_shape.append(jax.ShapeDtypeStruct((micros, length, hidden), low))
-            out_specs.append(by_block)
-        else:
-            out_shape.append(jax.ShapeDtypeStruct((micros,) + entry[0], entry[1]))
-            out_specs.append(by_micro(*entry[0]))
+    by_block = pl.BlockSpec((1, length, block), lambda m, s: (m, 0, jnp.minimum(s, last)))
+    heads, pairs = wq.shape[1], wk.shape[1]
+    columns = [width, width, width, hidden, hidden, heads, pairs, pairs, width, width, width]
+    specs = [by_micro(length, width)] * 3 + [by_block] * 2
+    specs += [by_micro(length, heads)] + [by_micro(length, pairs)] * 2 + [whole(other)] * 3
+    out_shape = [jax.ShapeDtypeStruct((micros, length, size), low) for size in columns]
     out_shape.append(jax.ShapeDtypeStruct(gains.shape, wide))
-    out_specs.append(whole(gains))
+    row = pltpu.SemaphoreType.DMA((micros,))
+    swaps = pltpu.SemaphoreType.DMA((2 * micros, SEND_PIECES))
     return pl.pallas_call(
-        functools.partial(backward_kernel, own, micros),
+        functools.partial(backward_kernel, micros),
         grid=(micros, HIDDEN_STEPS + 1),
         out_shape=out_shape,
         in_specs=[
             whole(cotangents),
             whole(other),
+            whole(far_first),
             whole(gains),
             whole(tables),
+            pl.BlockSpec(memory_space=pl.ANY),
+            pl.BlockSpec(memory_space=pl.ANY),
             by_micro(length, width),
             by_micro(groups, 2 * length, LANES),
             by_micro(groups, length, LANES),
@@ -655,177 +782,348 @@
             streamed(wu),
             streamed(wd),
         ],
-        out_specs=out_specs,
+        out_specs=specs + [whole(gains)],
         scratch_shapes=[
             pltpu.VMEM((micros, length, width), low),
             pltpu.VMEM((micros, length, width), low),
+            pltpu.VMEM((2 * micros, length, width), low),
+            pltpu.VMEM(gains.shape, wide),
             pltpu.VMEM((length, width), low),
             pltpu.VMEM((2 * micros, length, width), low),
             pltpu.VMEM((length, width), wide),
             pltpu.VMEM((length, width), wide),
-            pltpu.SemaphoreType.DMA((2 * micros, SEND_PIECES)),
-            pltpu.SemaphoreType.DMA((2 * micros, SEND_PIECES)),
-            pltpu.SemaphoreType.DMA((micros,)),
-            pltpu.SemaphoreType.DMA((micros,)),
-            pltpu.SemaphoreType.DMA((micros,)),
-            pltpu.SemaphoreType.DMA((micros,)),
+            swaps,
+            swaps,
+            row,
+            row,
+            row,
+            row,
+            pltpu.SemaphoreType.DMA((2 * micros, 4)),
+            pltpu.SemaphoreType.DMA,
+            pltpu.SemaphoreType.DMA,
         ],
         compiler_params=pltpu.CompilerParams(
             collective_id=1, has_side_effects=True, vmem_limit_bytes=62 * MIB
         ),
-    )(cotangents, other, gains, tables, *record, wq, wk, wv, wo, wg, wu, wd)
-
-
-WINDOW = 4
-LAG = 3
-
-
-def halving_kernel(widths, blocks, bits, axis, *refs):
-    count = len(widths)
-    grads, outs = refs[:count], refs[count : 2 * count]
-    rest = refs[2 * count :]
-    local, got = rest[:count], rest[count : count + count * bits]
-    load_sem, send_sem, recv_sem = rest[count + count * bits :]
-    me = lax.axis_index(axis)
-    own = [lax.rem(lax.div(me, 2**bit), 2) for bit in range(bits)]
-    flip = [me + (1 - 2 * own[bit]) * 2**bit for bit in range(bits)]
-    greet([{axis: flip[bit]} for bit in range(bits)])
-    plain = list(range(bits))
-    orders = [plain] if bits < 2 else [plain, [1, 0] + plain[2:]]
-    chunks = []
-    for which, width in enumerate(widths):
-        for at in range(grads[which].shape[-1] // width):
-            chunks.append((which, at))
-    plans = [orders[number % len(orders)] for number in range(len(chunks))]
-
-    def place(fixed):
-        return tuple(fixed[bit] if bit in fixed else slice(None) for bit in reversed(range(bits)))
-
-    loads, sends = {}, {}
-
-    def send(number, level, source, bit):
-        which, at = chunks[number]
-        copy = pltpu.make_async_remote_copy(
-            src_ref=source,
-            dst_ref=got[which * bits + level].at[at],
-            send_sem=send_sem.at[number, level],
-            recv_sem=recv_sem.at[number, level],
-            device_id={axis: flip[bit]},
+    )(cotangents, other, far_first, gains, tables, n1, n2, *record, wq, wk, wv, wo, wg, wu, wd)
+
+
+BLOCKS = 8
+PART = 3 * LANES
+
+
+class Halving:
+    def __init__(self, bits, local, got, sems, outputs):
+        self.bits, self.local, self.got, self.sems, self.outputs = bits, local, got, sems, outputs
+        me = lax.axis_index("dp")
+        self.own = [lax.rem(lax.div(me, 2**bit), 2) for bit in range(bits)]
+        self.flip = [me + (1 - 2 * self.own[bit]) * 2**bit for bit in range(bits)]
+        plain = list(range(bits))
+        self.orders = [plain, [1, 0] + plain[2:] if bits > 1 else plain]
+
+    def copy(self, block, half, level):
+        order = self.orders[half]
+        done, now = order[:level], order[level]
+        spot = []
+        for bit in reversed(range(self.bits)):
+            if bit in done:
+                spot.append(self.own[bit])
+            else:
+                spot.append(1 - self.own[bit] if bit == now else slice(None))
+        return pltpu.make_async_remote_copy(
+            src_ref=self.local.at[(block, half) + tuple(spot)],
+            dst_ref=self.got[level].at[block, half],
+            send_sem=self.sems.at[block, half, level, 0],
+            recv_sem=self.sems.at[block, half, level, 1],
+            device_id={"dp": self.flip[now]},
             device_id_type=MESH,
         )
-        copy.start()
-        sends[number, level] = copy
-
-    def begin(number):
-        which, at = chunks[number]
-        first = plans[number][0]
-        columns = pl.ds(at * widths[which], widths[which])
-        send(
-            number,
-            0,
-            grads[which].at[place({first: 1 - own[first]}) + (slice(None), columns)],
-            first,
+
+    def begin(self, block):
+        for half in range(2):
+            self.copy(block, half, 0).start()
+
+    def advance(self, block, level):
+        for half in range(2):
+            order = self.orders[half]
+            self.copy(block, half, level).wait()
+            done = order[: level + 1]
+            left = [bit for bit in reversed(range(self.bits)) if bit not in done]
+            rows = self.local.shape[-2]
+            piece = 64 if rows % 64 == 0 else rows
+            for combo in range(2 ** len(left)):
+                fixed = {bit: (combo >> index) & 1 for index, bit in enumerate(left)}
+                from_spot = (block, half) + tuple(fixed[bit] for bit in left)
+                for bit in done:
+                    fixed[bit] = self.own[bit]
+                spot = (block, half) + tuple(fixed[bit] for bit in reversed(range(self.bits)))
+
+                def add(index, _):
+                    where = pl.ds(pl.multiple_of(index * piece, piece), piece)
+                    a = self.local[spot + (where, slice(None))].astype(jnp.float32)
+                    b = self.got[level][from_spot + (where, slice(None))].astype(jnp.float32)
+                    if level == self.bits - 1:
+                        self.outputs(block, half, where, (a + b).astype(jnp.bfloat16))
+                    else:
+                        self.local[spot + (where, slice(None))] = (a + b).astype(jnp.bfloat16)
+                    return 0
+
+                lax.fori_loop(0, rows // piece, add, 0)
+            if level < self.bits - 1:
+                self.copy(block, half, level + 1).start()
+
+
+def gradient_kernel(
+    bits,
+    micros,
+    n1_rows,
+    n2_rows,
+    g_rows,
+    low_rows,
+    low_own,
+    act_own,
+    dgate_own,
+    dup_own,
+    dq_own,
+    dk_own,
+    dv_own,
+    o_own,
+    n1_far,
+    n2_far,
+    g_far,
+    tables,
+    gain_in,
+    wq,
+    wk,
+    wv,
+    wo,
+    wg,
+    wu,
+    wd,
+    gate_out,
+    up_out,
+    down_out,
+    q_out,
+    k_out,
+    v_out,
+    o_out,
+    gain_out,
+    far_low,
+    heads_far,
+    local,
+    *rest,
+):
+    step = pl.program_id(0)
+    got, small_got = rest[:bits], rest[bits + 1 : 2 * bits + 1]
+    small = rest[bits]
+    far_sems, sems, small_sems = rest[2 * bits + 1 :]
+    tensor, data = lax.axis_index("tensor"), lax.axis_index("dp")
+    peers = lax.axis_size("dp")
+    partner = lax.rem(data + peers // 2, peers)
+    length, width = far_low.shape[1:]
+    size = width // 2
+    rows = local.shape[-2]
+    top = lax.div(data, peers // 2)
+    lanes = pl.ds(pl.multiple_of(top * size, LANES), size)
+    far = FarCopies(low_own, far_low, far_sems, partner)
+    count = local.shape[0]
+
+    def small_output(block, half, where, value):
+        gain_out[half, where, :] = value
+
+    def output(block, half, where, value):
+        if isinstance(block, int):
+            target, at = [
+                [(q_out, 0), (q_out, PART)],
+                [(k_out, 0), (v_out, 0)],
+                [(o_out, 0), (o_out, PART)],
+            ][block - BLOCKS][half]
+            target[where, at : at + PART] = value
+        else:
+            at = pl.ds(pl.multiple_of(block * 2 * LANES + half * LANES, LANES), LANES)
+            for index, target in enumerate((gate_out, up_out, down_out)):
+                target[where, at] = value[:, index * LANES : (index + 1) * LANES]
+
+    halving = Halving(bits, local, got, sems, output)
+    gains = Halving(bits, small, small_got, small_sems, small_output)
+
+    @pl.when(step == 0)
+    def _():
+        greet(
+            [{"tensor": 1 - tensor}, {"dp": partner}] + [{"dp": halving.flip[bit]} for bit in range(bits)]
         )
-        load = pltpu.make_async_copy(
-            grads[which].at[place({first: own[first]}) + (slice(None), columns)],
-            local[which].at[at],
-            load_sem.at[number],
+        for which in range(micros):
+            far.start(which)
+        small[...] = gain_in[...]
+        gains.begin(0)
+
+    def blocked(value):
+        return value.astype(jnp.bfloat16).reshape((2,) * bits + (rows, value.shape[1]))
+
+    @pl.when(step < BLOCKS)
+    def _():
+        n2, g = n2_far[...], g_far[...]
+        gate, up = dot(n2, wg[...]), dot(n2, wu[...])
+        d_act = dot(g, wd[...])
+        sig = jax.nn.sigmoid(gate)
+        act = (gate * sig * up).astype(jnp.bfloat16)
+        d_gate = (d_act * up * sig * (1.0 + gate * (1.0 - sig))).astype(jnp.bfloat16)
+        d_up = (d_act * gate * sig).astype(jnp.bfloat16)
+        parts = (
+            (n2_rows, dgate_own, n2_far, d_gate),
+            (n2_rows, dup_own, n2_far, d_up),
+            (g_rows, act_own, g_far, act),
         )
-        load.start()
-        loads[number] = load
-
-    def step(number, level):
-        which, at = chunks[number]
-        order = plans[number]
-        width = widths[which]
-        block = blocks[which]
-        if level == 0:
-            loads[number].wait()
-        sends[number, level].wait_recv()
-        done = order[: level + 1]
-        left = [bit for bit in reversed(range(bits)) if bit not in done]
-        received = got[which * bits + level].at[at]
-        axes = [bit for bit in reversed(range(bits)) if bit != order[0]]
-        rows = 64 if block % 64 == 0 else block
-        for combo in range(2 ** len(left)):
-            fixed = {bit: (combo >> index) & 1 for index, bit in enumerate(left)}
-            for bit in done:
-                fixed[bit] = own[bit]
-            spot = (at,) + tuple(fixed[bit] for bit in axes)
-            from_spot = tuple(fixed[bit] for bit in left)
-
-            def add(piece, _):
-                where = pl.ds(pl.multiple_of(piece * rows, rows), rows)
-                a = local[which][spot + (where, slice(None))].astype(jnp.float32)
-                b = received[from_spot + (where, slice(None))].astype(jnp.float32)
-                if level == bits - 1:
-                    outs[which][where, pl.ds(at * width, width)] = (a + b).astype(jnp.bfloat16)
-                else:
-                    local[which][spot + (where, slice(None))] = (a + b).astype(jnp.bfloat16)
+        for index, (left, right, left_far, right_far) in enumerate(parts):
+            total = over_rows(left[...], right[...]) + over_rows(left_far[:, lanes], right_far)
+            for half in range(2):
+                spot = (step, half) + (slice(None),) * (bits + 1)
+                local[spot + (slice(index * LANES, (index + 1) * LANES),)] = blocked(
+                    total[:, half * LANES : (half + 1) * LANES]
+                )
+        halving.begin(step)
+
+    @pl.when((step > 0) & (step <= BLOCKS))
+    def _():
+        halving.advance(step - 1, 0)
+
+    @pl.when((step >= BLOCKS) & (step < BLOCKS + micros))
+    def _():
+        which = step - BLOCKS
+        far.receive(which)
+        low = far_low[which]
+        n1 = n1_far[pl.ds(pl.multiple_of(which * length, length), length), :]
+        query, keys, values = dot(n1, wq[...]), dot(n1, wk[...]), dot(n1, wv[...])
+        d_mixed = dot(low, wo[...]).astype(jnp.bfloat16).astype(jnp.float32)
+        trig, causal = trig_and_mask(tables, length)
+        cosine, sine, cosine2, sine2 = trig
+        d_queries, d_keys, d_values, outs = [], [], [], []
+        for group in range(wk.shape[1] // HEAD_SIZE):
+            q = jnp.concatenate([spread(query, 2 * group), spread(query, 2 * group + 1)], axis=0)
+            q = turned(q, cosine2, sine2).astype(jnp.bfloat16)
+            k = turned(spread(keys, group), cosine, sine).astype(jnp.bfloat16)
+            v = spread(values, group).astype(jnp.bfloat16)
+            parts = attention_backward(d_mixed, group, q, k, v, trig, causal, True)
+            d_queries += parts[0]
+            d_keys.append(parts[1])
+            d_values.append(parts[2])
+            outs += parts[3]
+        at = 0
+        for item in (d_queries, d_keys, d_values, outs):
+            item = gathered(item).astype(jnp.bfloat16)
+            heads_far[which, :, at : at + item.shape[1]] = item
+            at += item.shape[1]
+
+    @pl.when(step == BLOCKS + micros)
+    def _():
+        low_far = far_low[:, :, lanes].reshape(micros * length, size)
+        right_far = heads_far[...].reshape(micros * length, heads_far.shape[2])
+        plan = [
+            (n1_rows, dq_own, 0),
+            (n1_rows, dq_own, PART),
+            (n1_rows, dk_own, 0),
+            (n1_rows, dv_own, 0),
+            (low_rows, o_own, 0),
+            (low_rows, o_own, PART),
+        ]
+        for index, (left, right, at) in enumerate(plan):
+            left_far = low_far if left is low_rows else n1_far[:, lanes]
+            total = over_rows(left[...], right[:, at : at + PART]) + over_rows(
+                left_far, right_far[:, index * PART : (index + 1) * PART]
+            )
+            local[BLOCKS + index // 2, index % 2] = blocked(total)
+            if index % 2:
+                halving.begin(BLOCKS + index // 2)
+        gains.advance(0, 0)
+        for level in range(1, bits):
+
+            def advanced(block, _):
+                halving.advance(block, level)
                 return 0
 
-            lax.fori_loop(0, block // rows, add, 0)
-        if level < bits - 1:
-            following = order[level + 1]
-            source = []
-            for bit in axes:
-                if bit in done:
-                    source.append(own[bit])
-                elif bit == following:
-                    source.append(1 - own[bit])
-                else:
-                    source.append(slice(None))
-            send(number, level + 1, local[which].at[(at,) + tuple(source)], following)
-
-    total = len(chunks)
-    for number in range(min(WINDOW, total)):
-        begin(number)
-    for tick in range(total + LAG * (bits - 1)):
+            lax.fori_loop(0, BLOCKS, advanced, 0)
+            gains.advance(0, level)
         for level in range(bits):
-            number = tick - LAG * level
-            if 0 <= number < total:
-                step(number, level)
-        if tick + WINDOW < total:
-            begin(tick + WINDOW)
-    for copy in sends.values():
-        copy.wait_send()
-
-
-def scattered(grads, axis, bits):
-    blocks = [grad.shape[0] // 2**bits for grad in grads]
-    widths = [next(w for w in (256, 384, 128) if grad.shape[1] % w == 0) for grad in grads]
-    shaped = [
-        grad.reshape((2,) * bits + (block, grad.shape[1])) for grad, block in zip(grads, blocks)
+            for block in range(BLOCKS, count):
+                halving.advance(block, level)
+
+
+def gradients(bits, n1_far, low_own, own, far, tables, gain, weights):
+    wq, wk, wv, wo, wg, wu, wd = weights
+    micros, length, width = low_own.shape
+    n1_rows, n2_rows, g_rows, low_rows, act, d_gate, d_up, d_q, d_k, d_v, mixed = own
+    n2_far, g_far = far
+    hidden = wg.shape[1]
+    block = hidden // BLOCKS
+    rows = width // 2 ** (bits + 1)
+    low = jnp.bfloat16
+    count = BLOCKS + (d_q.shape[1] + d_k.shape[1] + d_v.shape[1] + mixed.shape[1]) // (2 * PART)
+
+    def whole(array):
+        return pl.BlockSpec(array.shape, lambda s: (0,) * array.ndim, pipeline_mode=pl.Buffered(1))
+
+    def streamed(array):
+        return pl.BlockSpec((array.shape[0], block), lambda s: (0, jnp.minimum(s, BLOCKS - 1)))
+
+    any_space = pl.BlockSpec(memory_space=pl.ANY)
+    args = [
+        (n1_rows, whole),
+        (n2_rows, whole),
+        (g_rows, whole),
+        (low_rows, whole),
+        (low_own, None),
+        (act, streamed),
+        (d_gate, streamed),
+        (d_up, streamed),
+        (d_q, whole),
+        (d_k, whole),
+        (d_v, whole),
+        (mixed, whole),
+        (n1_far, whole),
+        (n2_far, whole),
+        (g_far, whole),
+        (tables, whole),
+        (gain, whole),
+        (wq, whole),
+        (wk, whole),
+        (wv, whole),
+        (wo, whole),
+        (wg, streamed),
+        (wu, streamed),
+        (wd, streamed),
     ]
-    pieces = [grad.shape[1] // width for grad, width in zip(grads, widths)]
+    sizes = [hidden] * 3 + [d_q.shape[1], d_k.shape[1], d_v.shape[1], mixed.shape[1]]
+    out_shape = [jax.ShapeDtypeStruct((rows, size), low) for size in sizes]
+    small_rows = gain.shape[-2]
+    out_shape.append(jax.ShapeDtypeStruct((2, small_rows, LANES), low))
+
+    def levels(lead, tail):
+        return [pltpu.VMEM(lead + (2,) * (bits - 1 - level) + tail, low) for level in range(bits)]
+
     scratch = [
-        pltpu.VMEM((piece,) + (2,) * (bits - 1) + (block, width), jnp.bfloat16)
-        for piece, block, width in zip(pieces, blocks, widths)
+        pltpu.VMEM((micros, length, width), low),
+        pltpu.VMEM((micros, length, (count - BLOCKS) * 2 * PART), low),
+        pltpu.VMEM((count, 2) + (2,) * bits + (rows, PART), low),
     ]
-    for piece, block, width in zip(pieces, blocks, widths):
-        for level in range(bits):
-            scratch.append(
-                pltpu.VMEM((piece,) + (2,) * (bits - 1 - level) + (block, width), jnp.bfloat16)
-            )
-    total = sum(pieces)
+    scratch += levels((count, 2), (rows, PART))
+    scratch.append(pltpu.VMEM((1, 2) + (2,) * bits + (small_rows, LANES), low))
+    scratch += levels((1, 2), (small_rows, LANES))
     scratch += [
-        pltpu.SemaphoreType.DMA((total,)),
-        pltpu.SemaphoreType.DMA((total, bits)),
-        pltpu.SemaphoreType.DMA((total, bits)),
+        pltpu.SemaphoreType.DMA((micros, 4)),
+        pltpu.SemaphoreType.DMA((count, 2, bits, 2)),
+        pltpu.SemaphoreType.DMA((1, 2, bits, 2)),
     ]
     return pl.pallas_call(
-        functools.partial(halving_kernel, widths, blocks, bits, axis),
-        out_shape=[
-            jax.ShapeDtypeStruct((block, grad.shape[1]), jnp.bfloat16)
-            for grad, block in zip(grads, blocks)
-        ],
-        in_specs=[pl.BlockSpec(memory_space=pl.ANY)] * len(grads),
-        out_specs=[pl.BlockSpec(memory_space=pltpu.VMEM)] * len(grads),
+        functools.partial(gradient_kernel, bits, micros),
+        grid=(BLOCKS + micros + 1,),
+        out_shape=out_shape,
+        in_specs=[any_space if spec is None else spec(array) for array, spec in args],
+        out_specs=[whole(shape) for shape in out_shape],
         scratch_shapes=scratch,
         compiler_params=pltpu.CompilerParams(
-            collective_id=2, has_side_effects=True, vmem_limit_bytes=60 * MIB
+            collective_id=2, has_side_effects=True, vmem_limit_bytes=63 * MIB
         ),
-    )(*shaped)
+    )(*(array for array, _ in args))
 
 
 def body(
@@ -849,7 +1147,7 @@
         w_up[0],
         down_weight[0],
     )
-    micros, _, length, width = inputs.shape
+    _, _, length, width = inputs.shape
     gains = norm_scales[0].T
     tables = jnp.asarray(rope_tables(length))
     cots = cotangents[:, 0]
@@ -867,46 +1165,45 @@
         up,
         act,
         other,
+        far_first,
     ) = forward(inputs[:, 0], cots, gains, tables, weights)
-    grad, g, low, d_gate, d_up, d_q, d_k, d_v, gain = backward(
-        cots, other, gains, tables, (hidden, q, k, v, middle, gate, up), weights
+    grad, g, low, d_gate, d_up, d_q, d_k, d_v, n1_far, n2_far, g_far, gain = backward(
+        cots, other, far_first, gains, tables, n1, n2, (hidden, q, k, v, middle, gate, up), weights
     )
     peers = lax.axis_size("dp")
     bits = peers.bit_length() - 2
     top = lax.div(lax.axis_index("dp"), peers // 2)
 
-    def rows_of(values):
-        flat = values.reshape(-1, values.shape[-1])
-        size = flat.shape[-1] // 2
-        return lax.dynamic_slice_in_dim(flat, top * size, size, 1)
-
     def flat(values):
         return values.reshape(-1, values.shape[-1])
+
+    def rows_of(values):
+        return lax.dynamic_slice_in_dim(flat(values), top * (width // 2), width // 2, 1)
 
     gain_rows = lax.dynamic_slice_in_dim(gain, top * (width // 2), width // 2, 1).T
     gain_rows = gain_rows.astype(jnp.bfloat16).reshape(peers // 2, -1)
     gain_size = gain_rows.shape[1]
-    gain_rows = jnp.pad(gain_rows, ((0, 0), (0, 16 * LANES - gain_size))).reshape(-1, LANES)
-    n1_rows, n2_rows, low_rows, g_rows = rows_of(n1), rows_of(n2), rows_of(low), rows_of(g)
-    grads = [
-        over_rows(n2_rows, flat(d_gate)),
-        over_rows(n2_rows, flat(d_up)),
-        over_rows(g_rows, flat(act)),
-        over_rows(n1_rows, flat(d_q)),
-        over_rows(n1_rows, flat(d_k)),
-        over_rows(n1_rows, flat(d_v)),
-        over_rows(low_rows, flat(mixed)),
+    gain_rows = jnp.pad(gain_rows, ((0, 0), (0, 16 * LANES - gain_size)))
+    gain_rows = gain_rows.reshape((2,) * bits + (16, LANES))
+    gain_rows = jnp.stack([gain_rows, jnp.zeros_like(gain_rows)])[None]
+    *shards, small = gradients(
+        bits,
+        flat(n1_far),
+        low,
+        (rows_of(n1), rows_of(n2), rows_of(g), rows_of(low))
+        + tuple(flat(item) for item in (act, d_gate, d_up, d_q, d_k, d_v, mixed)),
+        (flat(n2_far), flat(g_far)),
+        tables,
         gain_rows,
-    ]
-    shards = scattered([item.astype(jnp.bfloat16) for item in grads], "dp", bits)
-    shards = [shard.astype(jnp.float32) for shard in shards]
-    grad_scales = shards[7].reshape(-1)[:gain_size].reshape(1, -1, 2)
+        weights,
+    )
+    grad_scales = small[0].astype(jnp.float32).reshape(-1)[:gain_size].reshape(1, -1, 2)
     grad_gate, grad_up, grad_down, grad_query, grad_key, grad_value, grad_proj = (
-        shard[None] for shard in shards[:7]
+        shard.astype(jnp.float32)[None] for shard in shards
     )
     return (
-        result[:micros][None, :, None],
-        grad[:micros][None, :, None],
+        result[None, :, None],
+        grad[None, :, None],
         grad_scales,
         grad_query,
         grad_key,

time: 393 us -> 366 us (0.931)
  matrix products: 24.8 us -> 0 us
  Pallas kernels: 353 us -> 346 us
    dot_general x7 -> x0, matrix products: 24.8 us -> none  [over_rows(): lax.dot_general(left, right, (((0,), (0,)), ((), ())), preferred_element_...]
    pallas_call x3, Pallas kernels: 353 us -> 346 us  [the longest x1 153 us: gradients(): pl.pallas_call(functools.partial(gradient_kernel, bits, micros), grid=(BL...]
    dynamic_slice x0 -> x2, local copies, waits for them, and re-layouts: none -> 4.01 us  [rows_of(): lax.dynamic_slice_in_dim(flat(values), top * (width // 2), width // 2, 1)]
    broadcast_in_dim x4 -> x7, other arithmetic: 6.78 us -> 8.35 us  [body(): shard.astype(jnp.float32)[None]]
where the time goes in v4:
time: 366 us
  Pallas kernels  346 us (95%)
  local copies, waits for them, and re-layouts  9.72 us (3%)
  other arithmetic  9.01 us (2%)
    pallas_call x1, Pallas kernels, gradients(): pl.pallas_call(functools.partial(gradient_kernel, bits, micros), grid=(BL...  153 us
    pallas_call x1, Pallas kernels, backward(): pl.pallas_call(functools.partial(backward_kernel, micros), grid=(micros,...  113 us
    pallas_call x1, Pallas kernels, forward(): pl.pallas_call(functools.partial(forward_kernel, micros), grid=(micros, H...  80.1 us
    broadcast_in_dim x7, other arithmetic, body(): shard.astype(jnp.float32)[None]  8.35 us

profile of v4, /device:TPU:0, one launch (start us, length us, event | category | flops | bytes accessed | tf_op | source)
XLA Modules:
  0.0 365.6 jit_solution(5853255686955790450)
XLA Ops:
  0.6 80.1 %shard_map.186 = (bf16[2,256,1536]{2,1,0:T(8,128)(2,1)}, bf16[2,256,1536]{2,1,0:T(8,128)(2,1)}, bf16[2,256,1536]{2,1,0:T(8,128)(2,1)}, bf16[2,4,512,128]{3,2,1,0...) custom-call(bf16[2,256,1536]{2,1,0:T(8,128)(2,1)} %bitcast.90, ...), custom_call_target="tpu_custom_call" | custom-call | tf_op jit(solution)/shard_map/pallas_call | solution.py:682
  80.7 113.1 %shard_map.187 = (bf16[2,256,1536]{2,1,0:T(8,128)(2,1)}, bf16[2,256,1536]{2,1,0:T(8,128)(2,1)}, bf16[2,256,1536]{2,1,0:T(8,128)(2,1)}, bf16[2,256,2048]{2,1,0:T(...) custom-call(bf16[2,256,1536]{2,1,0:T(8,128)(2,1)} %bitcast.83, ...), custom_call_target="tpu_custom_call" | custom-call | tf_op jit(solution)/shard_map/pallas_call | solution.py:758
  193.9 0.0 copy-start
  193.9 0.0 copy-start.1
  193.9 2.8 constant_dynamic-slice_fusion
  196.6 0.0 copy-done
  196.7 0.0 copy-done.1
  196.7 1.2 constant_dynamic-slice_fusion.2
  197.9 0.7 fusion
  198.6 0.2 copy.24
  198.8 0.3 reshape.91
  199.1 0.6 pad_bitcast_fusion.gain_in
  199.7 152.9 %shard_map.188 = (bf16[192,2048]{1,0:T(8,128)(2,1)}, bf16[192,2048]{1,0:T(8,128)(2,1)}, bf16[192,2048]{1,0:T(8,128)(2,1)}, bf16[192,768]{1,0:T(8,128)(2,1)}, bf1...) custom-call(bf16[512,768]{1,0:T(8,128)(2,1)} %get-tuple-element.101.n1, ...), custom_call_target="tpu_custom_call" | custom-call | tf_op jit(solution)/shard_map/pallas_call | solution.py:1116
  352.6 0.0 copy-start.5
  352.6 2.5 bitcast_convert_fusion
  355.1 0.0 copy-done.5
  355.2 1.3 bitcast_convert_fusion.1
  356.5 0.0 copy-done.4
  356.5 1.3 bitcast_convert_fusion.2
  357.8 0.0 copy-done.7
  357.8 0.9 bitcast_convert_fusion.3
  358.7 0.0 copy-done.6
  358.7 0.9 bitcast_convert_fusion.4
  359.5 0.7 bitcast_convert_fusion.5
  360.3 0.0 copy-done.8
  360.3 0.7 bitcast_convert_fusion.6
  361.0 0.7 slice_convert_fusion
  361.7 0.1 reshape.95
  361.8 0.7 copy.27
  362.5 1.1 copy.31
  363.6 0.8 copy-done.3
  364.5 1.1 copy.32
  (11 shorter events, 0.0 us)
Async XLA Ops:
  193.9 2.8 copy-start
  193.9 2.8 copy-start.1
  352.6 2.5 copy-start.5
  355.1 1.3 copy-start.4
  356.5 1.3 copy-start.7
  356.5 2.2 copy-start.6
  356.5 3.0 copy-start.9
  357.8 2.5 copy-start.8
  357.8 4.7 %copy-start.2 = (bf16[2,256,1536]{2,1,0:T(8,128)(2,1)S(1)}, bf16[2,256,1536]{2,1,0:T(8,128)(2,1)}, u32[]{:S(2)}) copy-start(bf16[2,256,1536]{2,1,0:T(8,128)(2,1)} %get-tuple-element.44) | copy-start | bytes 4718596
  362.5 2.0 copy-start.3
